TPU v7x, 8 devices: a whole 2x2x1 slice. The times are simulated.
8 devices in a mesh: inst: 1 (over z), qy: 2 (over y), qx: 4 (over x, core).
Axes of the slice: x: 2, y: 2, z: 1, core: 2. Of those that a mesh axis runs over, the one named last changes fastest.
Arguments:
- cost: float32 [2097152], P(('inst', 'qy', 'qx'))
- gamma: float32 [2, 3], P('inst')
- beta: float32 [2, 3], P('inst')
Outputs:
- output 1: float32 [2], P('inst')
- output 2: float32 [2, 6], P('inst')
All inputs are finite; a program needn't handle non-finite values.
Results may differ from a plain program's by a relative error of at most 0.001.
Values sent between devices are 32-bit elements.
A program may use at most 1 GiB of HBM per device.

v0:
```python
import jax
import jax.numpy as jnp
from jax import lax
from jax.sharding import PartitionSpec as P

LANE_BITS = 7
LANE_WIDTH = 128


def flip_grid(amplitudes, qubit):
    if qubit < LANE_BITS:
        shift = 2 ** qubit
        position = lax.broadcasted_iota(jnp.int32, (LANE_WIDTH,), 0)
        axis_pos = amplitudes.ndim - 1
    else:
        shift = 2 ** (qubit - LANE_BITS)
        position = lax.broadcasted_iota(jnp.int32, (amplitudes.shape[-2], 1), 0)
        axis_pos = amplitudes.ndim - 2
    upper = (position & shift) != 0
    return jnp.where(upper, jnp.roll(amplitudes, shift, axis=axis_pos), jnp.roll(amplitudes, -shift, axis=axis_pos))


def partner_tables(mesh):
    tables = []
    for axis_name in ('qx', 'qy'):
        width = mesh.shape[axis_name]
        for bit_pos in range(width.bit_length() - 1):
            tables.append((axis_name, [(index, index ^ (1 << bit_pos)) for index in range(width)]))
    return tables


def inverse_step(four_amps, partner, cos_b, sin_b):
    psi_re, psi_im, lam_re, lam_im = four_amps
    term = jnp.sum(lam_re * partner[1] - lam_im * partner[0], axis=(1, 2))
    updated = (cos_b * psi_re - sin_b * partner[1], cos_b * psi_im + sin_b * partner[0], cos_b * lam_re - sin_b * partner[3], cos_b * lam_im + sin_b * partner[2])
    return updated, term


def solution(mesh):
    partners = partner_tables(mesh)
    global_count = len(partners)
    group_axes = ('qy', 'qx')

    def device_fn(cost, gamma, beta):
        local_size = cost.shape[0]
        local_count = local_size.bit_length() - 1
        row_count = local_size // LANE_WIDTH
        num_sets, num_layers = gamma.shape
        start_amp = 2.0 ** (-0.5 * (local_count + global_count))
        cost_grid = cost.reshape(1, row_count, LANE_WIDTH)
        gamma_grid = gamma[:, :, None, None]
        half_cos = jnp.cos(0.5 * beta)[:, :, None, None]
        half_sin = jnp.sin(0.5 * beta)[:, :, None, None]
        psi_re = jnp.full((num_sets, row_count, LANE_WIDTH), start_amp, jnp.float32)
        psi_im = jnp.zeros_like(psi_re)
        phase_saved = []
        for layer in range(num_layers):
            phase = gamma_grid[:, layer] * cost_grid
            cos_p = jnp.cos(phase)
            sin_p = jnp.sin(phase)
            phase_saved.append((cos_p, sin_p))
            psi_re, psi_im = psi_re * cos_p + psi_im * sin_p, psi_im * cos_p - psi_re * sin_p
            cos_b = half_cos[:, layer]
            sin_b = half_sin[:, layer]
            for qubit in range(local_count):
                flip_re = flip_grid(psi_re, qubit)
                flip_im = flip_grid(psi_im, qubit)
                psi_re, psi_im = cos_b * psi_re + sin_b * flip_im, cos_b * psi_im - sin_b * flip_re
            for axis_name, pair_list in partners:
                partner = lax.ppermute(jnp.stack([psi_re, psi_im]), axis_name, pair_list)
                psi_re, psi_im = cos_b * psi_re + sin_b * partner[1], cos_b * psi_im - sin_b * partner[0]
        energy_part = jnp.sum(cost_grid * (psi_re * psi_re + psi_im * psi_im), axis=(1, 2))
        four_amps = (psi_re, psi_im, cost_grid * psi_re, cost_grid * psi_im)
        gamma_grads = [None] * num_layers
        beta_grads = [None] * num_layers
        for layer in reversed(range(num_layers)):
            cos_b = half_cos[:, layer]
            sin_b = half_sin[:, layer]
            beta_term = jnp.zeros((num_sets,), jnp.float32)
            for qubit in range(local_count):
                flips = [flip_grid(amplitudes, qubit) for amplitudes in four_amps]
                four_amps, term = inverse_step(four_amps, flips, cos_b, sin_b)
                beta_term = beta_term + term
            for axis_name, pair_list in partners:
                partner = lax.ppermute(jnp.stack(list(four_amps)), axis_name, pair_list)
                four_amps, term = inverse_step(four_amps, partner, cos_b, sin_b)
                beta_term = beta_term + term
            psi_re, psi_im, lam_re, lam_im = four_amps
            beta_grads[layer] = beta_term
            gamma_grads[layer] = 2.0 * jnp.sum(cost_grid * (lam_re * psi_im - lam_im * psi_re), axis=(1, 2))
            if layer > 0:
                cos_p, sin_p = phase_saved[layer]
                four_amps = (psi_re * cos_p - psi_im * sin_p, psi_im * cos_p + psi_re * sin_p, lam_re * cos_p - lam_im * sin_p, lam_im * cos_p + lam_re * sin_p)
        grad_rows = jnp.stack(gamma_grads + beta_grads, axis=1)
        totals = lax.psum(jnp.concatenate([energy_part[:, None], grad_rows], axis=1), group_axes)
        return totals[:, 0], totals[:, 1:]

    cost_spec = P(('inst', 'qy', 'qx'))
    angle_spec = P('inst', None)
    return jax.shard_map(device_fn, mesh=mesh, in_specs=(cost_spec, angle_spec, angle_spec), out_specs=(P('inst'), angle_spec), check_vma=False)
```

profile of v0, /device:TPU:0, one launch (start us, length us, event | category | flops | bytes accessed | tf_op | source)
XLA Modules:
  0.0 4030.7 jit_solution(10783502731276104908)
XLA Ops:
  213.1 45.8 %fusion.340 = f32[1,2,2048,128]{3,2,1,0:T(8,128)} fusion(f32[1,2,1792,128]{3,2,1,0:T(8,128)} %get-tuple-element.2094, f32[1,2,256,128]{3,2,1,0:T(8,128)} %get-tuple-element.2088, f32[1,2,256,128]{3,2,1,0:T(8,128)} %get-tuple-element.2089, f32[1,2,1792,128]{3,2,1,0:T(8,128)} %get-tuple-element.2092, f32[1,2,1536,128]{3,2,1,0:T(8,128)} %get-tuple-element.2096, ...), kind=kLoop, calls=%fused_computation.481 | loop fusion | flops 56623104 | bytes 74470168 | tf_op jit(solution)/shard_map/sub | solution.py:68
  258.9 45.9 %fusion.304 = f32[1,2,2048,128]{3,2,1,0:T(8,128)} fusion(f32[1,2,1792,128]{3,2,1,0:T(8,128)} %get-tuple-element.1964, f32[1,2,256,128]{3,2,1,0:T(8,128)} %get-tuple-element.1968, f32[1,2,256,128]{3,2,1,0:T(8,128)S(1)} %get-tuple-element.1967, f32[1,2,1792,128]{3,2,1,0:T(8,128)} %get-tuple-element.1963, f32[1,2,1536,128]{3,2,1,0:T(8,128)} %get-tuple-element.1956, ...), kind=kLoop, calls=%fused_computation.427 | loop fusion | flops 56623104 | bytes 74470168 | tf_op jit(solution)/shard_map/add | solution.py:68
  318.8 90.9 %collective-permute-done.1 = f32[2,2,2048,128]{3,2,1,0:T(8,128)S(1)} collective-permute-done((f32[2,2,2048,128]{3,2,1,0:T(8,128)S(1)}, f32[2,2,2048,128]{3,2,1,0:T(8,128)S(1)}, u32[]{:S(2)}, u32[]{:S(2)}) %collective-permute-start.1) | collective-permute-done | bytes 4194336 | tf_op jit(solution)/shard_map/ppermute | solution.py:70
  414.1 90.3 %collective-permute-done.2 = f32[2,2,2048,128]{3,2,1,0:T(8,128)S(1)} collective-permute-done((f32[2,2,2048,128]{3,2,1,0:T(8,128)S(1)}, f32[2,2,2048,128]{3,2,1,0:T(8,128)S(1)}, u32[]{:S(2)}, u32[]{:S(2)}) %collective-permute-start.2) | collective-permute-done | bytes 4194336 | tf_op jit(solution)/shard_map/ppermute | solution.py:70
  709.4 45.8 %fusion.456 = f32[1,2,2048,128]{3,2,1,0:T(8,128)} fusion(f32[1,2,1792,128]{3,2,1,0:T(8,128)} %get-tuple-element.1700, f32[1,2,256,128]{3,2,1,0:T(8,128)} %get-tuple-element.1704, f32[1,2,256,128]{3,2,1,0:T(8,128)} %get-tuple-element.1703, f32[1,2,1792,128]{3,2,1,0:T(8,128)} %get-tuple-element.1699, f32[1,2,1536,128]{3,2,1,0:T(8,128)} %get-tuple-element.1692, ...), kind=kLoop, calls=%fused_computation.651 | loop fusion | flops 59768832 | bytes 82858792 | tf_op jit(solution)/shard_map/add | solution.py:68
  755.1 45.8 %fusion.492 = f32[1,2,2048,128]{3,2,1,0:T(8,128)} fusion(f32[1,2,1792,128]{3,2,1,0:T(8,128)} %get-tuple-element.1824, f32[1,2,256,128]{3,2,1,0:T(8,128)S(1)} %get-tuple-element.1828, f32[1,2,256,128]{3,2,1,0:T(8,128)} %get-tuple-element.1829, f32[1,2,1792,128]{3,2,1,0:T(8,128)} %get-tuple-element.1825, f32[1,2,1536,128]{3,2,1,0:T(8,128)} %get-tuple-element.1686, ...), kind=kLoop, calls=%fused_computation.705 | loop fusion | flops 59768832 | bytes 82858792 | tf_op jit(solution)/shard_map/sub | solution.py:68
  813.1 91.2 %collective-permute-done.4 = f32[2,2,2048,128]{3,2,1,0:T(8,128)S(1)} collective-permute-done((f32[2,2,2048,128]{3,2,1,0:T(8,128)S(1)}, f32[2,2,2048,128]{3,2,1,0:T(8,128)S(1)}, u32[]{:S(2)}, u32[]{:S(2)}) %collective-permute-start.4) | collective-permute-done | bytes 4194336 | tf_op jit(solution)/shard_map/ppermute | solution.py:70
  908.4 90.3 %collective-permute-done.5 = f32[2,2,2048,128]{3,2,1,0:T(8,128)S(1)} collective-permute-done((f32[2,2,2048,128]{3,2,1,0:T(8,128)S(1)}, f32[2,2,2048,128]{3,2,1,0:T(8,128)S(1)}, u32[]{:S(2)}, u32[]{:S(2)}) %collective-permute-start.5) | collective-permute-done | bytes 4194336 | tf_op jit(solution)/shard_map/ppermute | solution.py:70
  1202.3 45.9 %fusion.639 = f32[1,2,2048,128]{3,2,1,0:T(8,128)} fusion(f32[1,2,1792,128]{3,2,1,0:T(8,128)} %get-tuple-element.1550, f32[1,2,256,128]{3,2,1,0:T(8,128)} %get-tuple-element.1544, f32[1,2,256,128]{3,2,1,0:T(8,128)} %get-tuple-element.1545, f32[1,2,1792,128]{3,2,1,0:T(8,128)} %get-tuple-element.1548, f32[1,2,1536,128]{3,2,1,0:T(8,128)} %get-tuple-element.1552, ...), kind=kLoop, calls=%fused_computation.924 | loop fusion | flops 59768832 | bytes 82858792 | tf_op jit(solution)/shard_map/sub | solution.py:68
  1248.3 46.1 %fusion.603 = f32[1,2,2048,128]{3,2,1,0:T(8,128)} fusion(f32[1,2,1792,128]{3,2,1,0:T(8,128)} %get-tuple-element.1420, f32[1,2,256,128]{3,2,1,0:T(8,128)S(1)} %get-tuple-element.1424, f32[1,2,256,128]{3,2,1,0:T(8,128)S(1)} %get-tuple-element.1423, f32[1,2,1792,128]{3,2,1,0:T(8,128)} %get-tuple-element.1419, f32[1,2,1536,128]{3,2,1,0:T(8,128)} %get-tuple-element.1412, ...), kind=kLoop, calls=%fused_computation.870 | loop fusion | flops 59768832 | bytes 82858792 | tf_op jit(solution)/shard_map/add | solution.py:68
  1311.5 91.2 %collective-permute-done.7 = f32[2,2,2048,128]{3,2,1,0:T(8,128)S(1)} collective-permute-done((f32[2,2,2048,128]{3,2,1,0:T(8,128)S(1)}, f32[2,2,2048,128]{3,2,1,0:T(8,128)S(1)}, u32[]{:S(2)}, u32[]{:S(2)}) %collective-permute-start.7) | collective-permute-done | bytes 4194336 | tf_op jit(solution)/shard_map/ppermute | solution.py:70
  1405.0 90.3 %collective-permute-done.8 = f32[2,2,2048,128]{3,2,1,0:T(8,128)S(1)} collective-permute-done((f32[2,2,2048,128]{3,2,1,0:T(8,128)S(1)}, f32[2,2,2048,128]{3,2,1,0:T(8,128)S(1)}, u32[]{:S(2)}, u32[]{:S(2)}) %collective-permute-start.8) | collective-permute-done | bytes 4194336 | tf_op jit(solution)/shard_map/ppermute | solution.py:70
  1530.3 16.8 subtract_reduce_fusion.19
  1571.4 15.7 subtract_reduce_fusion.18
  1612.4 15.9 subtract_reduce_fusion.17
  1653.1 15.6 subtract_reduce_fusion.16
  1693.8 16.1 subtract_reduce_fusion.15
  1937.7 181.0 %collective-permute-done.10 = f32[4,2,2048,128]{3,2,1,0:T(8,128)} collective-permute-done((f32[4,2,2048,128]{3,2,1,0:T(8,128)S(1)}, f32[4,2,2048,128]{3,2,1,0:T(8,128)}, u32[]{:S(2)}, u32[]{:S(2)}) %collective-permute-start.10) | collective-permute-done | bytes 8388640 | tf_op jit(solution)/shard_map/ppermute | solution.py:85
  2130.6 180.3 %collective-permute-done.11 = f32[4,2,2048,128]{3,2,1,0:T(8,128)S(1)} collective-permute-done((f32[4,2,2048,128]{3,2,1,0:T(8,128)S(1)}, f32[4,2,2048,128]{3,2,1,0:T(8,128)S(1)}, u32[]{:S(2)}, u32[]{:S(2)}) %collective-permute-start.11) | collective-permute-done | bytes 8388640 | tf_op jit(solution)/shard_map/ppermute | solution.py:85
  2453.7 15.7 subtract_reduce_fusion.38
  2494.2 15.9 subtract_reduce_fusion.37
  2535.2 16.1 subtract_reduce_fusion.36
  2779.3 181.0 %collective-permute-done.13 = f32[4,2,2048,128]{3,2,1,0:T(8,128)} collective-permute-done((f32[4,2,2048,128]{3,2,1,0:T(8,128)S(1)}, f32[4,2,2048,128]{3,2,1,0:T(8,128)}, u32[]{:S(2)}, u32[]{:S(2)}) %collective-permute-start.13) | collective-permute-done | bytes 8388640 | tf_op jit(solution)/shard_map/ppermute | solution.py:85
  2972.2 180.3 %collective-permute-done.14 = f32[4,2,2048,128]{3,2,1,0:T(8,128)S(1)} collective-permute-done((f32[4,2,2048,128]{3,2,1,0:T(8,128)S(1)}, f32[4,2,2048,128]{3,2,1,0:T(8,128)S(1)}, u32[]{:S(2)}, u32[]{:S(2)}) %collective-permute-start.14) | collective-permute-done | bytes 8388640 | tf_op jit(solution)/shard_map/ppermute | solution.py:85
  3213.5 15.6 subtract_reduce_fusion.61
  3254.5 15.8 subtract_reduce_fusion.60
  3295.7 15.6 subtract_reduce_fusion.59
  3336.2 15.7 subtract_reduce_fusion.58
  3377.3 16.0 subtract_reduce_fusion.57
  3619.3 181.0 %collective-permute-done.16 = f32[4,2,2048,128]{3,2,1,0:T(8,128)} collective-permute-done((f32[4,2,2048,128]{3,2,1,0:T(8,128)S(1)}, f32[4,2,2048,128]{3,2,1,0:T(8,128)}, u32[]{:S(2)}, u32[]{:S(2)}) %collective-permute-start.16) | collective-permute-done | bytes 8388640 | tf_op jit(solution)/shard_map/ppermute | solution.py:85
  3819.8 175.1 %collective-permute-done.17 = f32[4,2,2048,128]{3,2,1,0:T(8,128)} collective-permute-done((f32[4,2,2048,128]{3,2,1,0:T(8,128)}, f32[4,2,2048,128]{3,2,1,0:T(8,128)}, u32[]{:S(2)}, u32[]{:S(2)}) %collective-permute-start.17) | collective-permute-done | bytes 8388640 | tf_op jit(solution)/shard_map/ppermute | solution.py:85
  4005.9 23.2 psum.7
  (2239 shorter events, 1892.7 us)
Async XLA Ops:
  0.7 1247.6 %copy-start.503 = (pred[128]{0:T(512)(128)(4,1)}, pred[128]{0:T(512)(128)(4,1)S(1)}, u32[]{:S(2)}) copy-start(pred[128]{0:T(512)(128)(4,1)S(1)} %get-tuple-element.2153) | copy-start | bytes 388
  0.7 1247.6 %copy-start.507 = (pred[128]{0:T(512)(128)(4,1)}, pred[128]{0:T(512)(128)(4,1)S(1)}, u32[]{:S(2)}) copy-start(pred[128]{0:T(512)(128)(4,1)S(1)} %get-tuple-element.2154) | copy-start | bytes 388
  0.7 258.1 %copy-start.406 = (pred[2048]{0:T(1024)(128)(4,1)}, pred[2048]{0:T(1024)(128)(4,1)S(1)}, u32[]{:S(2)}) copy-start(pred[2048]{0:T(1024)(128)(4,1)S(1)} %get-tuple-element.2155) | copy-start | bytes 6148
  0.8 258.1 %copy-start.412 = (pred[2048]{0:T(1024)(128)(4,1)}, pred[2048]{0:T(1024)(128)(4,1)S(1)}, u32[]{:S(2)}) copy-start(pred[2048]{0:T(1024)(128)(4,1)S(1)} %get-tuple-element.2156) | copy-start | bytes 6148
  20.0 484.4 %copy-start.368 = (f32[2]{0:T(128)}, f32[2]{0:T(128)S(1)}, u32[]{:S(2)}) copy-start(f32[2]{0:T(128)S(1)} %get-tuple-element.29) | copy-start | bytes 28
  20.0 484.4 %copy-start.371 = (f32[2]{0:T(128)}, f32[2]{0:T(128)S(1)}, u32[]{:S(2)}) copy-start(f32[2]{0:T(128)S(1)} %get-tuple-element.2147) | copy-start | bytes 28
  307.5 7.7 collective-permute-start
  316.0 93.8 %collective-permute-start.1 = (f32[2,2,2048,128]{3,2,1,0:T(8,128)S(1)}, f32[2,2,2048,128]{3,2,1,0:T(8,128)S(1)}, u32[]{:S(2)}, u32[]{:S(2)}) collective-permute-start(f32[2,2,2048,128]{3,2,1,0:T(8,128)S(1)} %pad_maximum_fusion.10), channel_id=1, source_target_pairs={{0,2},{1,3},{2,0},{3,1},{4,6},{5,7},{6,4},{7,5}} | collective-permute-start | bytes 12582920 | tf_op jit(solution)/shard_map/ppermute | solution.py:70
  412.4 92.0 %collective-permute-start.2 = (f32[2,2,2048,128]{3,2,1,0:T(8,128)S(1)}, f32[2,2,2048,128]{3,2,1,0:T(8,128)S(1)}, u32[]{:S(2)}, u32[]{:S(2)}) collective-permute-start(f32[2,2,2048,128]{3,2,1,0:T(8,128)S(1)} %pad_maximum_fusion.11), channel_id=1, source_target_pairs={{0,4},{4,0},{1,5},{5,1},{2,6},{6,2},{3,7},{7,3}} | collective-permute-start | bytes 12582920 | tf_op jit(solution)/shard_map/ppermute | solution.py:70
  803.6 7.2 collective-permute-start.3
  811.6 92.6 %collective-permute-start.4 = (f32[2,2,2048,128]{3,2,1,0:T(8,128)S(1)}, f32[2,2,2048,128]{3,2,1,0:T(8,128)S(1)}, u32[]{:S(2)}, u32[]{:S(2)}) collective-permute-start(f32[2,2,2048,128]{3,2,1,0:T(8,128)S(1)} %pad_maximum_fusion.13), channel_id=1, source_target_pairs={{0,2},{1,3},{2,0},{3,1},{4,6},{5,7},{6,4},{7,5}} | collective-permute-start | bytes 12582920 | tf_op jit(solution)/shard_map/ppermute | solution.py:70
  906.9 91.8 %collective-permute-start.5 = (f32[2,2,2048,128]{3,2,1,0:T(8,128)S(1)}, f32[2,2,2048,128]{3,2,1,0:T(8,128)S(1)}, u32[]{:S(2)}, u32[]{:S(2)}) collective-permute-start(f32[2,2,2048,128]{3,2,1,0:T(8,128)S(1)} %pad_maximum_fusion.14), channel_id=1, source_target_pairs={{0,4},{4,0},{1,5},{5,1},{2,6},{6,2},{3,7},{7,3}} | collective-permute-start | bytes 12582920 | tf_op jit(solution)/shard_map/ppermute | solution.py:70
  1297.2 7.2 collective-permute-start.6
  1310.0 92.6 %collective-permute-start.7 = (f32[2,2,2048,128]{3,2,1,0:T(8,128)S(1)}, f32[2,2,2048,128]{3,2,1,0:T(8,128)S(1)}, u32[]{:S(2)}, u32[]{:S(2)}) collective-permute-start(f32[2,2,2048,128]{3,2,1,0:T(8,128)S(1)} %pad_maximum_fusion.16), channel_id=1, source_target_pairs={{0,2},{1,3},{2,0},{3,1},{4,6},{5,7},{6,4},{7,5}} | collective-permute-start | bytes 12582920 | tf_op jit(solution)/shard_map/ppermute | solution.py:70
  1403.5 91.8 %collective-permute-start.8 = (f32[2,2,2048,128]{3,2,1,0:T(8,128)S(1)}, f32[2,2,2048,128]{3,2,1,0:T(8,128)S(1)}, u32[]{:S(2)}, u32[]{:S(2)}) collective-permute-start(f32[2,2,2048,128]{3,2,1,0:T(8,128)S(1)} %pad_maximum_fusion.17), channel_id=1, source_target_pairs={{0,4},{4,0},{1,5},{5,1},{2,6},{6,2},{3,7},{7,3}} | collective-permute-start | bytes 12582920 | tf_op jit(solution)/shard_map/ppermute | solution.py:70
  1914.7 13.2 collective-permute-start.9
  1933.0 185.8 %copy-start.159 = (f32[2,2048,128]{2,1,0:T(8,128)S(1)}, f32[2,2048,128]{2,1,0:T(8,128)}, u32[]{:S(2)}) copy-start(f32[2,2048,128]{2,1,0:T(8,128)} %get-tuple-element.429) | copy-start | bytes 6291460
  1936.2 182.5 %collective-permute-start.10 = (f32[4,2,2048,128]{3,2,1,0:T(8,128)S(1)}, f32[4,2,2048,128]{3,2,1,0:T(8,128)}, u32[]{:S(2)}, u32[]{:S(2)}) collective-permute-start(f32[4,2,2048,128]{3,2,1,0:T(8,128)S(1)} %pad_maximum_fusion.1), channel_id=1, source_target_pairs={{0,2},{1,3},{2,0},{3,1},{4,6},{5,7},{6,4},{7,5}} | collective-permute-start | bytes 25165832 | tf_op jit(solution)/shard_map/ppermute | solution.py:85
  2126.4 184.4 %copy-start.4 = (f32[262144]{0:T(1024)S(1)}, f32[262144]{0:T(1024)}, u32[]{:S(2)}) copy-start(f32[262144]{0:T(1024)} %param.3) | copy-start | bytes 3145732
  2126.4 184.4 %copy-start.162 = (f32[2,2048,128]{2,1,0:T(8,128)S(1)}, f32[2,2048,128]{2,1,0:T(8,128)}, u32[]{:S(2)}) copy-start(f32[2,2048,128]{2,1,0:T(8,128)} %get-tuple-element.453) | copy-start | bytes 6291460
  2126.4 184.4 %copy-start.163 = (f32[2,2048,128]{2,1,0:T(8,128)S(1)}, f32[2,2048,128]{2,1,0:T(8,128)}, u32[]{:S(2)}) copy-start(f32[2,2048,128]{2,1,0:T(8,128)} %get-tuple-element.454) | copy-start | bytes 6291460
  2126.4 184.4 %copy-start.586 = (f32[2]{0:T(128)S(1)}, f32[2]{0:T(128)}, u32[]{:S(2)}) copy-start(f32[2]{0:T(128)} %get-tuple-element.30) | copy-start | bytes 28
  2129.1 181.8 %collective-permute-start.11 = (f32[4,2,2048,128]{3,2,1,0:T(8,128)S(1)}, f32[4,2,2048,128]{3,2,1,0:T(8,128)S(1)}, u32[]{:S(2)}, u32[]{:S(2)}) collective-permute-start(f32[4,2,2048,128]{3,2,1,0:T(8,128)S(1)} %pad_maximum_fusion.2), channel_id=1, source_target_pairs={{0,4},{4,0},{1,5},{5,1},{2,6},{6,2},{3,7},{7,3}} | collective-permute-start | bytes 25165832 | tf_op jit(solution)/shard_map/ppermute | solution.py:85
  2756.2 13.2 collective-permute-start.12
  2774.6 185.8 %copy-start.160 = (f32[2,2048,128]{2,1,0:T(8,128)S(1)}, f32[2,2048,128]{2,1,0:T(8,128)}, u32[]{:S(2)}) copy-start(f32[2,2048,128]{2,1,0:T(8,128)} %get-tuple-element.435) | copy-start | bytes 6291460
  2777.8 182.5 %collective-permute-start.13 = (f32[4,2,2048,128]{3,2,1,0:T(8,128)S(1)}, f32[4,2,2048,128]{3,2,1,0:T(8,128)}, u32[]{:S(2)}, u32[]{:S(2)}) collective-permute-start(f32[4,2,2048,128]{3,2,1,0:T(8,128)S(1)} %pad_maximum_fusion.4), channel_id=1, source_target_pairs={{0,2},{1,3},{2,0},{3,1},{4,6},{5,7},{6,4},{7,5}} | collective-permute-start | bytes 25165832 | tf_op jit(solution)/shard_map/ppermute | solution.py:85
  2968.1 184.4 %copy-start.165 = (f32[2,2048,128]{2,1,0:T(8,128)S(1)}, f32[2,2048,128]{2,1,0:T(8,128)}, u32[]{:S(2)}) copy-start(f32[2,2048,128]{2,1,0:T(8,128)} %get-tuple-element.450) | copy-start | bytes 6291460
  2968.1 184.4 %copy-start.584 = (f32[2]{0:T(128)S(1)}, f32[2]{0:T(128)}, u32[]{:S(2)}) copy-start(f32[2]{0:T(128)} %get-tuple-element.31) | copy-start | bytes 28
  2970.7 181.8 %collective-permute-start.14 = (f32[4,2,2048,128]{3,2,1,0:T(8,128)S(1)}, f32[4,2,2048,128]{3,2,1,0:T(8,128)S(1)}, u32[]{:S(2)}, u32[]{:S(2)}) collective-permute-start(f32[4,2,2048,128]{3,2,1,0:T(8,128)S(1)} %pad_maximum_fusion.5), channel_id=1, source_target_pairs={{0,4},{4,0},{1,5},{5,1},{2,6},{6,2},{3,7},{7,3}} | collective-permute-start | bytes 25165832 | tf_op jit(solution)/shard_map/ppermute | solution.py:85
  3595.6 13.2 collective-permute-start.15
  3617.8 182.5 %collective-permute-start.16 = (f32[4,2,2048,128]{3,2,1,0:T(8,128)S(1)}, f32[4,2,2048,128]{3,2,1,0:T(8,128)}, u32[]{:S(2)}, u32[]{:S(2)}) collective-permute-start(f32[4,2,2048,128]{3,2,1,0:T(8,128)S(1)} %pad_maximum_fusion.7), channel_id=1, source_target_pairs={{0,2},{1,3},{2,0},{3,1},{4,6},{5,7},{6,4},{7,5}} | collective-permute-start | bytes 25165832 | tf_op jit(solution)/shard_map/ppermute | solution.py:85
  3813.2 181.8 %collective-permute-start.17 = (f32[4,2,2048,128]{3,2,1,0:T(8,128)}, f32[4,2,2048,128]{3,2,1,0:T(8,128)}, u32[]{:S(2)}, u32[]{:S(2)}) collective-permute-start(f32[4,2,2048,128]{3,2,1,0:T(8,128)} %pad_maximum_fusion.8), channel_id=1, source_target_pairs={{0,4},{4,0},{1,5},{5,1},{2,6},{6,2},{3,7},{7,3}} | collective-permute-start | bytes 25165832 | tf_op jit(solution)/shard_map/ppermute | solution.py:85
  (678 other events, 4407.9 us)
where the time goes:
time: 4040 us; the launch traced here: 4030 us
  waiting for transfers between devices  1680 us (42%)
  other arithmetic  1250 us (31%)
  local copies, waits for them, and re-layouts  1040 us (26%)
    ppermute x9, waiting for transfers between devices, device_fn(): partner = lax.ppermute(jnp.stack(list(four_amps)), axis_name, pair_list)  1120 us
    ppermute x9, waiting for transfers between devices, device_fn(): partner = lax.ppermute(jnp.stack([psi_re, psi_im]), axis_name, pair_list)  565 us
    reduce_sum x61, other arithmetic, inverse_step(): term = jnp.sum(lam_re * partner[1] - lam_im * partner[0], axis=(1, 2))  537 us
    slice x418, local copies, waits for them, and re-layouts, flip_grid(): jnp.roll(amplitudes, shift, axis=axis_pos)  476 us
    concatenate x174, local copies, waits for them, and re-layouts, flip_grid(): jnp.roll(amplitudes, shift, axis=axis_pos)  367 us
    add x30, other arithmetic, device_fn(): cos_b * psi_re + sin_b * flip_im  217 us
    sub x29, other arithmetic, device_fn(): cos_b * psi_im - sin_b * flip_re  212 us
    unnamed x1384, local copies, waits for them, and re-layouts  164 us
  transfers between devices with their start and end apart: 18, of which 18 were waited for; matrix products, arithmetic and copies ran while one was open for 0% of the time, Pallas kernels for 0%

commit v1 on v0

v1 whole, which is shorter than its diff:
```python
import functools
import math
import jax
import jax.numpy as jnp
from jax import lax
from jax.experimental import pallas as pl
from jax.experimental.pallas import tpu as pltpu
from jax.sharding import PartitionSpec as P

F32 = jnp.float32
BF16 = jnp.bfloat16
NK = 32
RB = 128
LN = 128
CH = 8
NCH = RB // CH
GC = 4
KG = 4
MESH = pl.DeviceIdType.MESH
LOCAL = 20


def popcount(value, bits):
    total = value % 2
    for bit in range(1, bits):
        total = total + (value // 2 ** bit) % 2
    return total


def sincos(theta):
    turns = jnp.round(theta * (1.0 / math.pi))
    red = theta - turns * 3.140625
    red = red - turns * 9.67502593994140625e-4
    red = red - turns * 1.509957990978376432e-7
    half = turns * 0.5
    sign = 1.0 - 4.0 * (half - jnp.floor(half))
    sq = red * red
    sin_p = 2.634850360e-06
    sin_p = sin_p * sq - 1.982277571e-04
    sin_p = sin_p * sq + 8.333242483e-03
    sin_p = sin_p * sq - 1.666666597e-01
    sin_v = (sin_p * sq * red + red) * sign
    cos_p = -2.629828691e-07
    cos_p = cos_p * sq + 2.477462031e-05
    cos_p = cos_p * sq - 1.388865233e-03
    cos_p = cos_p * sq + 4.166665940e-02
    cos_p = cos_p * sq - 4.999999996e-01
    cos_v = (cos_p * sq + 1.0) * sign
    return sin_v, cos_v


def butterfly(items, bits):
    shape = items.shape
    for bit in bits:
        step = 1 << bit
        pairs = items.reshape((shape[0] // (2 * step), 2, step) + shape[1:])
        first = pairs[:, 0]
        second = pairs[:, 1]
        items = jnp.stack([first + second, first - second], axis=1).reshape(shape)
    return items


def split_dot(values, table):
    high = values.astype(BF16)
    rest = values - high.astype(F32)
    mid = rest.astype(BF16)
    low = (rest - mid.astype(F32)).astype(BF16)
    parts = jnp.concatenate([high, mid, low], axis=1)
    return jnp.dot(parts, table, preferred_element_type=F32)


def kernel(cost_ref, gamma_ref, beta_ref, out_ref, cost_all, work, recv, hats, phis, had, tmp, dtab, wtab, acc, part, peers,
           own_s, own_r, rel_s, rel_r, core_s, core_r, ex_s, ex_r, fin_s, fin_r, credit):
    pos_y = lax.axis_index('qy')
    pos_b = lax.axis_index('qx')
    pos_x = pos_b // 2
    core = pos_b % 2
    other = 1 - core
    near_core = {'qy': pos_y, 'qx': pos_x * 2 + other}
    near_x = {'qy': pos_y, 'qx': (1 - pos_x) * 2 + core}
    near_y = {'qy': 1 - pos_y, 'qx': pos_b}
    near_yc = {'qy': 1 - pos_y, 'qx': pos_x * 2 + other}

    barrier = pltpu.get_barrier_semaphore()
    for dev in (near_core, near_x, near_y, near_yc):
        pl.semaphore_signal(barrier, inc=1, device_id=dev, device_id_type=MESH)
    pl.semaphore_wait(barrier, 4)

    def slot(block_y, block_x, block_core, chunk):
        return cost_all.at[block_y, block_x, pl.ds(block_core * 16 + chunk * GC, GC)]

    def push(src, dst, send, rcv, dev):
        return pltpu.make_async_remote_copy(src_ref=src, dst_ref=dst, send_sem=send, recv_sem=rcv, device_id=dev, device_id_type=MESH)

    sends = []

    def go(copy):
        copy.start()
        sends.append(copy)

    for q in range(4):
        src = cost_ref.at[pl.ds(q * GC, GC)]
        dst = slot(pos_y, pos_x, core, q)
        go(push(src, dst, own_s.at[0, q], own_r.at[0, q], near_x))
        go(push(src, dst, own_s.at[1, q], own_r.at[1, q], near_y))
        go(push(src, dst, core_s.at[0, q], core_r.at[0, q], near_core))
    cost_all[pos_y, pos_x, pl.ds(core * 16, 16)] = cost_ref[...]

    row_i = lax.broadcasted_iota(jnp.int32, (256, 256), 0)
    col_i = lax.broadcasted_iota(jnp.int32, (256, 256), 1)
    bits = row_i & col_i
    bits = bits ^ (bits >> 4)
    bits = bits ^ (bits >> 2)
    bits = bits ^ (bits >> 1)
    had_v = (1 - 2 * (bits & 1)).astype(F32).astype(BF16)
    for part_i in range(3):
        had[pl.ds(part_i * 256, 256), :] = had_v
    lane_i = lax.broadcasted_iota(jnp.int32, (8, 256), 1)
    sub_i = lax.broadcasted_iota(jnp.int32, (8, 256), 0)
    ones = sub_i & 1
    for bit in range(1, 3):
        ones = ones + ((sub_i >> bit) & 1)
    for bit in range(8):
        ones = ones + ((lane_i >> bit) & 1)
    wtab[...] = (LOCAL - 2 * ones).astype(F32)
    acc[...] = jnp.zeros_like(acc)

    for q in range(4):
        block = slot(pos_y, 1 - pos_x, core, q)
        push(block, block, own_s.at[0, q], own_r.at[0, q], near_x).wait_recv()
        go(push(block, block, core_s.at[1, q], core_r.at[1, q], near_core))
        if q < 2:
            go(push(block, block, rel_s.at[q], rel_r.at[q], near_y))
        block = slot(1 - pos_y, pos_x, core, q)
        push(block, block, own_s.at[1, q], own_r.at[1, q], near_y).wait_recv()
        go(push(block, block, core_s.at[2, q], core_r.at[2, q], near_core))
        if q >= 2:
            go(push(block, block, rel_s.at[q], rel_r.at[q], near_x))
    for q in (0, 2, 1, 3):
        block = slot(1 - pos_y, 1 - pos_x, core, q)
        push(block, block, rel_s.at[q], rel_r.at[q], near_x).wait_recv()
        go(push(block, block, core_s.at[3, q], core_r.at[3, q], near_core))
    for q in range(4):
        for kind, (by, bx) in enumerate(((pos_y, pos_x), (pos_y, 1 - pos_x), (1 - pos_y, pos_x), (1 - pos_y, 1 - pos_x))):
            block = slot(by, bx, other, q)
            push(block, block, core_s.at[kind, q], core_r.at[kind, q], near_core).wait_recv()
    for copy in sends:
        copy.wait_send()

    def make_dtab(layer, sign):
        half = 0.5 * beta_ref[pos_y, layer]
        for pop in range(10):
            sin_v, cos_v = sincos(half * (wtab[...] - 2.0 * pop))
            dtab[0, pop] = cos_v * 2.0 ** -LOCAL
            dtab[1, pop] = sin_v * (sign * 2.0 ** -LOCAL)

    def half_angle(layer):
        return sincos(jnp.full((1, CH, LN), 0.5 * beta_ref[pos_y, layer], F32))

    def cost_half(layout, half, ks, rows):
        if layout == 0:
            return cost_all[core, half, ks, rows, :]
        return cost_all[half, core, ks, rows, :]

    def radix32(src, dst):
        dst[...] = butterfly(src[...], range(5))

    def chunk_of(ref, ri, half, i):
        return ref.at[ri, half, :, pl.ds(pl.multiple_of(i * CH, CH), CH), :]

    def rchunk_of(ri, i):
        return recv.at[ri, :, pl.ds(pl.multiple_of(i * CH, CH), CH), :]

    def exchange(i):
        rows = pl.ds(pl.multiple_of(i * CH, CH), CH)
        return push(work.at[:, other, :, rows, :], recv.at[:, :, rows, :], ex_s.at[i], ex_r.at[i], near_core)

    def inner(layer):
        def body(i, carry):
            for ri in range(2):
                for half in range(2):
                    items = butterfly(work[ri, half, i].reshape(16, 8, LN), range(3))
                    tmp[ri, half] = items.reshape(RB, LN)
            rows = []
            for ri in range(2):
                cols = []
                for half in range(2):
                    items = [tmp[ri, half, pl.ds(m, 16, stride=8), :].reshape(1, 2, 8, LN) for m in range(8)]
                    items = butterfly(jnp.concatenate(items, axis=0).reshape(16, 8, LN), range(4))
                    cols.append(items.reshape(RB, LN))
                rows.append(jnp.concatenate(cols, axis=1))
            first = split_dot(jnp.concatenate(rows, axis=0), had[...])
            re_v = first[:RB]
            im_v = first[RB:]
            pop_i = popcount(i, 5)
            if layer[1] < 0:
                prod = re_v * hats[layer[0], 1, i] - im_v * hats[layer[0], 0, i]
                sums = [None] * 5
                for m in range(16):
                    pop = bin(m).count('1')
                    piece = prod[8 * m:8 * m + 8]
                    sums[pop] = piece if sums[pop] is None else sums[pop] + piece
                flat = sums[0] + sums[1] + sums[2] + sums[3] + sums[4]
                tilt = sums[1] + 2.0 * sums[2] + 3.0 * sums[3] + 4.0 * sums[4]
                weight = wtab[...] - 2.0 * pop_i.astype(F32)
                total = weight * flat - 2.0 * tilt
                acc[1 + layer[0]] += total[:, :LN] + total[:, LN:]
            cos_d = jnp.concatenate([dtab[0, pop_i + bin(m).count('1')] for m in range(16)], axis=0)
            sin_d = jnp.concatenate([dtab[1, pop_i + bin(m).count('1')] for m in range(16)], axis=0)
            re_v, im_v = re_v * cos_d + im_v * sin_d, im_v * cos_d - re_v * sin_d
            if layer[1] > 0:
                hats[layer[0], 0, i] = re_v
                hats[layer[0], 1, i] = im_v
            turned = jnp.concatenate([re_v, im_v], axis=0)
            second = split_dot(turned, had[...])
            for ri in range(2):
                for half in range(2):
                    items = second[RB * ri:RB * ri + RB, LN * half:LN * half + LN]
                    items = butterfly(items.reshape(16, 8, LN), range(4)).reshape(8, 16, LN)
                    for m in range(8):
                        tmp[ri, half, pl.ds(m, 16, stride=8), :] = items[m]
            for ri in range(2):
                for half in range(2):
                    items = butterfly(tmp[ri, half].reshape(16, 8, LN), range(3))
                    work[ri, half, i] = items.reshape(RB, LN)
            return carry

        lax.fori_loop(0, NK, body, 0)

    def last_rows(i):
        for ri in range(2):
            for half in range(2):
                ref = chunk_of(work, ri, half, i)
                radix32(ref, ref)

    def pieces(i, kg):
        return pl.ds(kg * KG, KG), pl.ds(pl.multiple_of(i * CH, CH), CH)

    def mix_pair(own_re, own_im, oth_re, oth_im, cos_b, sin_b):
        return (cos_b * own_re + sin_b * oth_im, cos_b * own_im - sin_b * oth_re,
                cos_b * oth_re + sin_b * own_im, cos_b * oth_im - sin_b * own_re)

    def first_rows(i, received):
        for ri in range(2):
            ref = chunk_of(work, ri, core, i)
            radix32(ref, ref)
            dst = chunk_of(work, ri, other, i)
            radix32(rchunk_of(ri, i) if received else dst, dst)

    for layer in range(3):
        layout = layer % 2
        make_dtab(layer, 1.0)
        sin_b, cos_b = half_angle(layer)
        angle = gamma_ref[pos_y, layer]
        if layer > 0:
            pl.semaphore_wait(credit, 1)

        def send_body(i, carry):
            if layer > 0:
                last_rows(i)

            def point(kg, carry2):
                ks, rows = pieces(i, kg)
                state = []
                for half in range(2):
                    sin_p, cos_p = sincos(angle * cost_half(layout, half, ks, rows))
                    if layer == 0:
                        scale = 2.0 ** (-0.5 * (LOCAL + 1))
                        re_v = cos_p * scale
                        im_v = sin_p * -scale
                    else:
                        re_v = work[0, half, ks, rows, :]
                        im_v = work[1, half, ks, rows, :]
                        re_v, im_v = re_v * cos_p + im_v * sin_p, im_v * cos_p - re_v * sin_p
                        phis[layer - 1, 0, half, ks, rows, :] = re_v
                        phis[layer - 1, 1, half, ks, rows, :] = im_v
                    state += [re_v, im_v]
                state = mix_pair(*state, cos_b, sin_b)
                for half in range(2):
                    for ri in range(2):
                        work[ri, half, ks, rows, :] = state[2 * half + ri]
                return carry2

            lax.fori_loop(0, NK // KG, point, 0)
            exchange(i).start()
            return carry

        lax.fori_loop(0, NCH, send_body, 0)

        def take_body(i, carry):
            exchange(i).wait()
            first_rows(i, True)
            return carry

        lax.fori_loop(0, NCH, take_body, 0)
        pl.semaphore_signal(credit, inc=1, device_id=near_core, device_id_type=MESH)
        inner((layer, 1))

    def turn_body(i, carry):
        last_rows(i)

        def point(kg, total):
            ks, rows = pieces(i, kg)
            for half in range(2):
                cost_v = cost_half(1, half, ks, rows)
                re_v = work[0, half, ks, rows, :]
                im_v = work[1, half, ks, rows, :]
                lam_re = cost_v * re_v
                lam_im = cost_v * im_v
                work[0, half, ks, rows, :] = lam_re
                work[1, half, ks, rows, :] = lam_im
                total = total + jnp.sum(lam_re * re_v + lam_im * im_v, axis=0)
            return total

        acc[0] += lax.fori_loop(0, NK // KG, point, jnp.zeros((CH, LN), F32))
        first_rows(i, False)
        return carry

    lax.fori_loop(0, NCH, turn_body, 0)

    for layer in (2, 1, 0):
        layout = layer % 2
        make_dtab(layer, -1.0)
        sin_b, cos_b = half_angle(layer)
        angle = gamma_ref[pos_y, layer]
        inner((layer, -1))
        pl.semaphore_wait(credit, 1)

        def back_send(i, carry):
            last_rows(i)
            exchange(i).start()
            return carry

        lax.fori_loop(0, NCH, back_send, 0)

        def back_take(i, carry):
            exchange(i).wait()

            def point(kg, sums):
                ks, rows = pieces(i, kg)
                beta_sum, gamma_sum = sums
                own_re = work[0, core, ks, rows, :]
                own_im = work[1, core, ks, rows, :]
                oth_re = recv[0, ks, rows, :]
                oth_im = recv[1, ks, rows, :]
                lam = mix_pair(own_re, own_im, oth_re, oth_im, cos_b, -sin_b)
                lams = {0: lam[:2], 1: lam[2:]}
                phi = []
                costs = []
                waves = []
                for side in (core, other):
                    cost_v = cost_half(layout, side, ks, rows)
                    costs.append(cost_v)
                    sin_p, cos_p = sincos(angle * cost_v)
                    waves.append((sin_p, cos_p))
                    if layer == 0:
                        scale = 2.0 ** (-0.5 * (LOCAL + 1))
                        phi.append((cos_p * scale, sin_p * -scale))
                    else:
                        phi.append((phis[layer - 1, 0, side, ks, rows, :], phis[layer - 1, 1, side, ks, rows, :]))
                for side in range(2):
                    lam_re, lam_im = lams[side]
                    gamma_sum = gamma_sum + jnp.sum(costs[side] * (lam_re * phi[side][1] - lam_im * phi[side][0]), axis=0)
                    beta_sum = beta_sum + jnp.sum(lam_re * phi[1 - side][1] - lam_im * phi[1 - side][0], axis=0)
                    if layer > 0:
                        sin_p, cos_p = waves[side]
                        where = core if side == 0 else other
                        work[0, where, ks, rows, :] = lam_re * cos_p - lam_im * sin_p
                        work[1, where, ks, rows, :] = lam_im * cos_p + lam_re * sin_p
                return beta_sum, gamma_sum

            zero = jnp.zeros((CH, LN), F32)
            beta_sum, gamma_sum = lax.fori_loop(0, NK // KG, point, (zero, zero))
            acc[1 + layer] += beta_sum
            acc[4 + layer] += 2.0 * gamma_sum
            if layer > 0:
                first_rows(i, False)
            return carry

        lax.fori_loop(0, NCH, back_take, 0)
        if layer > 0:
            pl.semaphore_signal(credit, inc=1, device_id=near_core, device_id_type=MESH)

    order = (0, 4, 5, 6, 1, 2, 3)
    rows = [jnp.sum(acc[q], axis=0, keepdims=True) for q in order]
    part[...] = jnp.concatenate(rows + [jnp.zeros((1, LN), F32)], axis=0)
    peers[pos_y, core] = part[...]
    fins = [push(part, peers.at[pos_y, core], fin_s.at[0], fin_r.at[0], near_core),
            push(part, peers.at[pos_y, core], fin_s.at[1], fin_r.at[1], near_y),
            push(part, peers.at[pos_y, core], fin_s.at[2], fin_r.at[2], near_yc)]
    for copy in fins:
        copy.start()
    for copy in fins:
        copy.wait()
    for s in range(2):
        out_ref[s] = jnp.broadcast_to(jnp.sum(peers[s, 0] + peers[s, 1], axis=1, keepdims=True), (8, LN))


def solution(mesh):
    def device_fn(cost, gamma, beta):
        vmem = pl.BlockSpec(memory_space=pltpu.VMEM)
        smem = pl.BlockSpec(memory_space=pltpu.SMEM)
        dma = pltpu.SemaphoreType.DMA
        out = pl.pallas_call(
            kernel,
            out_shape=jax.ShapeDtypeStruct((2, 8, LN), F32),
            in_specs=[vmem, smem, smem],
            out_specs=vmem,
            scratch_shapes=[
                pltpu.VMEM((2, 2, NK, RB, LN), F32),
                pltpu.VMEM((2, 2, NK, RB, LN), F32),
                pltpu.VMEM((2, NK, RB, LN), F32),
                pltpu.VMEM((3, 2, NK, RB, 2 * LN), F32),
                pltpu.VMEM((2, 2, 2, NK, RB, LN), F32),
                pltpu.VMEM((768, 256), BF16),
                pltpu.VMEM((2, 2, RB, LN), F32),
                pltpu.VMEM((2, 10, 8, 256), F32),
                pltpu.VMEM((8, 256), F32),
                pltpu.VMEM((8, 8, LN), F32),
                pltpu.VMEM((8, LN), F32),
                pltpu.VMEM((2, 2, 8, LN), F32),
                dma((2, 4)), dma((2, 4)), dma((4,)), dma((4,)), dma((4, 4)), dma((4, 4)),
                dma((NCH,)), dma((NCH,)), dma((3,)), dma((3,)),
                pltpu.SemaphoreType.REGULAR,
            ],
            compiler_params=pltpu.CompilerParams(collective_id=0, has_side_effects=True, vmem_limit_bytes=67043328),
        )(cost.reshape(16, RB, LN), gamma, beta)
        return out[:, 0, 0], out[:, 1:7, 0]

    cost_spec = P(('inst', 'qy', 'qx'))
    angle_spec = P('inst', None)
    return jax.shard_map(device_fn, mesh=mesh, in_specs=(cost_spec, angle_spec, angle_spec), out_specs=(P('inst'), angle_spec), check_vma=False)
```

time: 4040 us -> 272 us (0.07)
  waiting for transfers between devices: 1680 us -> 0 us
  other arithmetic: 1250 us -> 0 us
  local copies, waits for them, and re-layouts: 1040 us -> 2.65 us
  Pallas kernels: 0 us -> 268 us
    ppermute x18 -> x0, waiting for transfers between devices: 1680 us -> none  [the longest x9 1120 us: device_fn(): partner = lax.ppermute(jnp.stack(list(four_amps)), axis_name, pair_list)]
    reduce_sum x62 -> x0, other arithmetic: 541 us -> none  [the longest x61 537 us: inverse_step(): term = jnp.sum(lam_re * partner[1] - lam_im * partner[0], axis=(1, 2))]
    slice x430 -> x2, local copies, waits for them, and re-layouts: 492 us -> 2.65 us  [device_fn(): return (out[:, 0, 0], out[:, 1:7, 0])]
    concatenate x187 -> x0, local copies, waits for them, and re-layouts: 386 us -> none  [the longest x174 367 us: flip_grid(): jnp.roll(amplitudes, shift, axis=axis_pos)]
    add x70 -> x0, other arithmetic: 331 us -> none  [the longest x30 217 us: device_fn(): cos_b * psi_re + sin_b * flip_im]
    sub x57 -> x0, other arithmetic: 313 us -> none  [the longest x29 212 us: device_fn(): cos_b * psi_im - sin_b * flip_re]
    pallas_call x0 -> x1, Pallas kernels: none -> 268 us  [device_fn(): pl.pallas_call(kernel, out_shape=jax.ShapeDtypeStruct((2, 8, LN), F32), i...]
    unnamed x1384 -> x0, local copies, waits for them, and re-layouts: 164 us -> none
  transfers between devices with their start and end apart: 18 -> 0, of which waited for: 18 -> 0; matrix products, arithmetic and copies ran while one was open for 0% -> 0% of each run, Pallas kernels for 0% -> 0%
where the time goes in v1:
time: 272 us
  Pallas kernels  268 us (99%)
    pallas_call x1, Pallas kernels, device_fn(): pl.pallas_call(kernel, out_shape=jax.ShapeDtypeStruct((2, 8, LN), F32), i...  268 us

profile of v1, /device:TPU:0, one launch (start us, length us, event | category | flops | bytes accessed | tf_op | source)
XLA Modules:
  0.0 271.6 jit_solution(17740410803006057752)
XLA Ops:
  0.6 268.3 %shard_map.50 = f32[2,8,128]{2,1,0:T(8,128)} custom-call(f32[16,128,128]{2,1,0:T(8,128)} %bitcast.1, f32[2,3]{1,0:T(2,128)} %gamma_ref.1, f32[2,3]{1,0:T(2,128)} %beta_ref.1), custom_call_target="tpu_custom_call" | custom-call | tf_op jit(solution)/shard_map/pallas_call | solution.py:404
  269.0 1.3 slice_reduce_fusion.1
  270.3 1.3 slice_reduce_fusion

commit v2 on v1

--- a/solution.py
+++ b/solution.py
@@ -15,9 +15,10 @@
 CH = 8
 NCH = RB // CH
 GC = 4
-KG = 4
+KG = 8
 MESH = pl.DeviceIdType.MESH
-LOCAL = 20
+QUBITS = 21
+ROWQ = 12
 
 
 def popcount(value, bits):
@@ -27,26 +28,22 @@
     return total
 
 
-def sincos(theta):
-    turns = jnp.round(theta * (1.0 / math.pi))
-    red = theta - turns * 3.140625
-    red = red - turns * 9.67502593994140625e-4
-    red = red - turns * 1.509957990978376432e-7
-    half = turns * 0.5
-    sign = 1.0 - 4.0 * (half - jnp.floor(half))
-    sq = red * red
-    sin_p = 2.634850360e-06
-    sin_p = sin_p * sq - 1.982277571e-04
-    sin_p = sin_p * sq + 8.333242483e-03
-    sin_p = sin_p * sq - 1.666666597e-01
-    sin_v = (sin_p * sq * red + red) * sign
-    cos_p = -2.629828691e-07
-    cos_p = cos_p * sq + 2.477462031e-05
-    cos_p = cos_p * sq - 1.388865233e-03
-    cos_p = cos_p * sq + 4.166665940e-02
-    cos_p = cos_p * sq - 4.999999996e-01
-    cos_v = (cos_p * sq + 1.0) * sign
-    return sin_v, cos_v
+def sincos(turns):
+    frac = turns - jnp.round(turns)
+    sq = frac * frac
+    sin_h = 1.098257528e-01
+    sin_h = sin_h * sq - 8.461123459e-01
+    sin_h = sin_h * sq + 3.606354339e+00
+    sin_h = sin_h * sq - 7.308245693e+00
+    sin_h = sin_h * sq + 4.442882919e+00
+    sin_h = sin_h * frac
+    cos_h = -3.450177884e-02
+    cos_h = cos_h * sq + 3.322516636e-01
+    cos_h = cos_h * sq - 1.888274957e+00
+    cos_h = cos_h * sq + 5.739881543e+00
+    cos_h = cos_h * sq - 6.978864110e+00
+    cos_h = cos_h * sq + 1.414213562e+00
+    return sin_h * cos_h, 1.0 - sin_h * sin_h
 
 
 def butterfly(items, bits):
@@ -60,16 +57,14 @@
     return items
 
 
-def split_dot(values, table):
+def split(values):
     high = values.astype(BF16)
     rest = values - high.astype(F32)
     mid = rest.astype(BF16)
-    low = (rest - mid.astype(F32)).astype(BF16)
-    parts = jnp.concatenate([high, mid, low], axis=1)
-    return jnp.dot(parts, table, preferred_element_type=F32)
-
-
-def kernel(cost_ref, gamma_ref, beta_ref, out_ref, cost_all, work, recv, hats, phis, had, tmp, dtab, wtab, acc, part, peers,
+    return high, mid, (rest - mid.astype(F32)).astype(BF16)
+
+
+def kernel(cost_ref, gamma_ref, beta_ref, out_ref, cost_all, work, recv, hats, phis, rot, flip, tmp, tmp2, lhs, dtab, wtab, acc, part, peers,
            own_s, own_r, rel_s, rel_r, core_s, core_r, ex_s, ex_r, fin_s, fin_r, credit):
     pos_y = lax.axis_index('qy')
     pos_b = lax.axis_index('qx')
@@ -104,25 +99,19 @@
         go(push(src, dst, own_s.at[0, q], own_r.at[0, q], near_x))
         go(push(src, dst, own_s.at[1, q], own_r.at[1, q], near_y))
         go(push(src, dst, core_s.at[0, q], core_r.at[0, q], near_core))
+
     cost_all[pos_y, pos_x, pl.ds(core * 16, 16)] = cost_ref[...]
 
     row_i = lax.broadcasted_iota(jnp.int32, (256, 256), 0)
     col_i = lax.broadcasted_iota(jnp.int32, (256, 256), 1)
-    bits = row_i & col_i
-    bits = bits ^ (bits >> 4)
-    bits = bits ^ (bits >> 2)
-    bits = bits ^ (bits >> 1)
-    had_v = (1 - 2 * (bits & 1)).astype(F32).astype(BF16)
-    for part_i in range(3):
-        had[pl.ds(part_i * 256, 256), :] = had_v
-    lane_i = lax.broadcasted_iota(jnp.int32, (8, 256), 1)
-    sub_i = lax.broadcasted_iota(jnp.int32, (8, 256), 0)
-    ones = sub_i & 1
-    for bit in range(1, 3):
-        ones = ones + ((sub_i >> bit) & 1)
-    for bit in range(8):
-        ones = ones + ((lane_i >> bit) & 1)
-    wtab[...] = (LOCAL - 2 * ones).astype(F32)
+    differ = row_i ^ col_i
+    single = (differ != 0) & ((differ & (differ - 1)) == 0)
+    flip_v = jnp.where(single, jnp.where(row_i > col_i, 1.0, -1.0), 0.0).astype(BF16)
+    flip[...] = flip_v
+    lane_i = lax.broadcasted_iota(jnp.int32, (8, LN), 1)
+    sub_i = lax.broadcasted_iota(jnp.int32, (8, LN), 0)
+    wtab[...] = (ROWQ - 2 * popcount(sub_i, 3)).astype(F32)
+    lane_ones = popcount(lane_i, 7)
     acc[...] = jnp.zeros_like(acc)
 
     for q in range(4):
@@ -148,14 +137,43 @@
         copy.wait_send()
 
     def make_dtab(layer, sign):
-        half = 0.5 * beta_ref[pos_y, layer]
+        half = (0.25 / math.pi) * beta_ref[pos_y, layer]
         for pop in range(10):
             sin_v, cos_v = sincos(half * (wtab[...] - 2.0 * pop))
-            dtab[0, pop] = cos_v * 2.0 ** -LOCAL
-            dtab[1, pop] = sin_v * (sign * 2.0 ** -LOCAL)
+            dtab[0, pop] = cos_v * 2.0 ** -ROWQ
+            dtab[1, pop] = sin_v * (sign * 2.0 ** -ROWQ)
 
     def half_angle(layer):
-        return sincos(jnp.full((1, CH, LN), 0.5 * beta_ref[pos_y, layer], F32))
+        return sincos(jnp.full((1, CH, LN), (0.25 / math.pi) * beta_ref[pos_y, layer], F32))
+
+    def make_rot(layer, sign):
+        sin_b, cos_b = sincos(jnp.full((8, 256), (0.25 / math.pi) * beta_ref[pos_y, layer], F32))
+        sin_b = sin_b * sign
+        cols = lax.broadcasted_iota(jnp.int32, (8, 256), 1)
+
+        def body(n, carry):
+            tiles = []
+            for sub in range(2):
+                lines = lax.broadcasted_iota(jnp.int32, (8, 256), 0) + n * 16 + sub * 8
+                delta = lines ^ cols
+                total = None
+                for bit in range(8):
+                    factor = jnp.where((delta >> bit) & 1 == 0, cos_b, jnp.where((lines >> bit) & 1 == 1, sin_b, -sin_b))
+                    total = factor if total is None else total * factor
+                tiles.append(total)
+            high, mid, low = split(jnp.concatenate(tiles, axis=0))
+            for m, piece in enumerate((high, mid, low)):
+                rot[pl.ds(pl.multiple_of(m * 256 + n * 16, 16), 16), :] = piece
+            return carry
+
+        lax.fori_loop(0, 16, body, 0)
+
+    def frame(ones):
+        turn = ones % 4
+        real = jnp.where(turn == 0, 1.0, jnp.where(turn == 2, -1.0, 0.0))
+        imag = jnp.where(turn == 1, -1.0, jnp.where(turn == 3, 1.0, 0.0))
+        scale = 2.0 ** (-0.5 * QUBITS)
+        return real[None] * scale, imag[None] * scale
 
     def cost_half(layout, half, ks, rows):
         if layout == 0:
@@ -175,26 +193,26 @@
         rows = pl.ds(pl.multiple_of(i * CH, CH), CH)
         return push(work.at[:, other, :, rows, :], recv.at[:, :, rows, :], ex_s.at[i], ex_r.at[i], near_core)
 
-    def inner(layer):
-        def body(i, carry):
+    def row_wave(i):
+        pop_i = popcount(jnp.asarray(i, jnp.int32), 5)
+        pops = [bin(m).count('1') for m in range(16)]
+        return [jnp.concatenate([dtab[n, pop_i + pop] for pop in pops], axis=0) for n in range(2)]
+
+    def stage_in(i, slot, layer, forward):
+        if forward:
+            cos_d, sin_d = row_wave(i)
+        for half in range(2):
+            pair = []
             for ri in range(2):
-                for half in range(2):
-                    items = butterfly(work[ri, half, i].reshape(16, 8, LN), range(3))
-                    tmp[ri, half] = items.reshape(RB, LN)
-            rows = []
-            for ri in range(2):
-                cols = []
-                for half in range(2):
-                    items = [tmp[ri, half, pl.ds(m, 16, stride=8), :].reshape(1, 2, 8, LN) for m in range(8)]
-                    items = butterfly(jnp.concatenate(items, axis=0).reshape(16, 8, LN), range(4))
-                    cols.append(items.reshape(RB, LN))
-                rows.append(jnp.concatenate(cols, axis=1))
-            first = split_dot(jnp.concatenate(rows, axis=0), had[...])
-            re_v = first[:RB]
-            im_v = first[RB:]
-            pop_i = popcount(i, 5)
-            if layer[1] < 0:
-                prod = re_v * hats[layer[0], 1, i] - im_v * hats[layer[0], 0, i]
+                items = butterfly(work[ri, half, i].reshape(16, 8, LN), range(3))
+                tmp[...] = items.reshape(RB, LN)
+                items = [tmp[pl.ds(m, 16, stride=8), :].reshape(1, 2, 8, LN) for m in range(8)]
+                pair.append(butterfly(jnp.concatenate(items, axis=0).reshape(16, 8, LN), range(4)).reshape(RB, LN))
+            re_v, im_v = pair
+            if forward:
+                pair = [re_v * cos_d + im_v * sin_d, im_v * cos_d - re_v * sin_d]
+            else:
+                prod = re_v * hats[layer, 1, half, i] - im_v * hats[layer, 0, half, i]
                 sums = [None] * 5
                 for m in range(16):
                     pop = bin(m).count('1')
@@ -202,30 +220,55 @@
                     sums[pop] = piece if sums[pop] is None else sums[pop] + piece
                 flat = sums[0] + sums[1] + sums[2] + sums[3] + sums[4]
                 tilt = sums[1] + 2.0 * sums[2] + 3.0 * sums[3] + 4.0 * sums[4]
-                weight = wtab[...] - 2.0 * pop_i.astype(F32)
-                total = weight * flat - 2.0 * tilt
-                acc[1 + layer[0]] += total[:, :LN] + total[:, LN:]
-            cos_d = jnp.concatenate([dtab[0, pop_i + bin(m).count('1')] for m in range(16)], axis=0)
-            sin_d = jnp.concatenate([dtab[1, pop_i + bin(m).count('1')] for m in range(16)], axis=0)
-            re_v, im_v = re_v * cos_d + im_v * sin_d, im_v * cos_d - re_v * sin_d
-            if layer[1] > 0:
-                hats[layer[0], 0, i] = re_v
-                hats[layer[0], 1, i] = im_v
-            turned = jnp.concatenate([re_v, im_v], axis=0)
-            second = split_dot(turned, had[...])
+                pop_i = popcount(jnp.asarray(i, jnp.int32), 5)
+                acc[1 + layer] += (wtab[...] - 2.0 * jnp.asarray(pop_i, F32)) * flat - 2.0 * tilt
             for ri in range(2):
-                for half in range(2):
-                    items = second[RB * ri:RB * ri + RB, LN * half:LN * half + LN]
-                    items = butterfly(items.reshape(16, 8, LN), range(4)).reshape(8, 16, LN)
-                    for m in range(8):
-                        tmp[ri, half, pl.ds(m, 16, stride=8), :] = items[m]
-            for ri in range(2):
-                for half in range(2):
-                    items = butterfly(tmp[ri, half].reshape(16, 8, LN), range(3))
-                    work[ri, half, i] = items.reshape(RB, LN)
-            return carry
-
-        lax.fori_loop(0, NK, body, 0)
+                for n, piece in enumerate(split(pair[ri])):
+                    lhs[slot, pl.ds(RB * ri, RB), pl.ds(2 * LN * n + LN * half, LN)] = piece
+
+    def stage_out(i, slot, layer, forward):
+        high = lhs[slot, :, 0:256]
+        mid = lhs[slot, :, 256:512]
+        low = lhs[slot, :, 512:768]
+        table = [rot[0:256], rot[256:512], rot[512:768]]
+        table = jnp.concatenate([table[0], table[1], table[2], table[0], table[1], table[0]], axis=0)
+        prod = jnp.dot(jnp.concatenate([high, high, high, mid, mid, low], axis=1), table, preferred_element_type=F32)
+        if not forward:
+            turned = jnp.dot(jnp.concatenate([high, mid, low], axis=1), jnp.concatenate([flip[...]] * 3, axis=0), preferred_element_type=F32)
+            total = None
+            for half in range(2):
+                for ri in range(2):
+                    piece = turned[RB * ri:RB * ri + RB, LN * half:LN * half + LN] * hats[layer, ri, half, i]
+                    piece = jnp.sum(piece.reshape(16, 8, LN), axis=0)
+                    total = piece if total is None else total + piece
+            acc[1 + layer] -= total
+            cos_d, sin_d = row_wave(i)
+        for half in range(2):
+            re_v = prod[:RB, LN * half:LN * half + LN]
+            im_v = prod[RB:, LN * half:LN * half + LN]
+            if forward:
+                hats[layer, 0, half, i] = re_v
+                hats[layer, 1, half, i] = im_v
+            else:
+                re_v, im_v = re_v * cos_d + im_v * sin_d, im_v * cos_d - re_v * sin_d
+            for ri, items in enumerate((re_v, im_v)):
+                items = butterfly(items.reshape(16, 8, LN), range(4)).reshape(8, 2, 8, LN)
+                for b6 in range(2):
+                    tmp2[64 * b6:64 * b6 + 64] = items[:, b6].reshape(64, LN)
+                items = [tmp2[pl.ds(m, 16, stride=8), :].reshape(2, 1, 8, LN) for m in range(8)]
+                items = butterfly(jnp.concatenate(items, axis=1).reshape(16, 8, LN), range(3))
+                work[ri, half, i] = items.reshape(RB, LN)
+
+    def inner(layer, forward):
+        stage_in(0, 0, layer, forward)
+
+        def body(p, carry):
+            stage_out(p, 0, layer, forward)
+            stage_in(p + 1, 0, layer, forward)
+            return carry
+
+        lax.fori_loop(0, NK - 1, body, 0)
+        stage_out(NK - 1, 0, layer, forward)
 
     def last_rows(i):
         for ri in range(2):
@@ -237,8 +280,8 @@
         return pl.ds(kg * KG, KG), pl.ds(pl.multiple_of(i * CH, CH), CH)
 
     def mix_pair(own_re, own_im, oth_re, oth_im, cos_b, sin_b):
-        return (cos_b * own_re + sin_b * oth_im, cos_b * own_im - sin_b * oth_re,
-                cos_b * oth_re + sin_b * own_im, cos_b * oth_im - sin_b * own_re)
+        return (cos_b * own_re + sin_b * oth_re, cos_b * own_im + sin_b * oth_im,
+                cos_b * oth_re - sin_b * own_re, cos_b * oth_im - sin_b * own_im)
 
     def first_rows(i, received):
         for ri in range(2):
@@ -250,8 +293,9 @@
     for layer in range(3):
         layout = layer % 2
         make_dtab(layer, 1.0)
+        make_rot(layer, 1.0)
         sin_b, cos_b = half_angle(layer)
-        angle = gamma_ref[pos_y, layer]
+        angle = (0.5 / math.pi) * gamma_ref[pos_y, layer]
         if layer > 0:
             pl.semaphore_wait(credit, 1)
 
@@ -265,9 +309,9 @@
                 for half in range(2):
                     sin_p, cos_p = sincos(angle * cost_half(layout, half, ks, rows))
                     if layer == 0:
-                        scale = 2.0 ** (-0.5 * (LOCAL + 1))
-                        re_v = cos_p * scale
-                        im_v = sin_p * -scale
+                        real, imag = frame(lane_ones + core + half)
+                        re_v = cos_p * real + sin_p * imag
+                        im_v = cos_p * imag - sin_p * real
                     else:
                         re_v = work[0, half, ks, rows, :]
                         im_v = work[1, half, ks, rows, :]
@@ -294,7 +338,7 @@
 
         lax.fori_loop(0, NCH, take_body, 0)
         pl.semaphore_signal(credit, inc=1, device_id=near_core, device_id_type=MESH)
-        inner((layer, 1))
+        inner(layer, True)
 
     def turn_body(i, carry):
         last_rows(i)
@@ -321,9 +365,11 @@
     for layer in (2, 1, 0):
         layout = layer % 2
         make_dtab(layer, -1.0)
+        make_rot(layer, -1.0)
         sin_b, cos_b = half_angle(layer)
-        angle = gamma_ref[pos_y, layer]
-        inner((layer, -1))
+        sin_b = sin_b * (2 * core - 1).astype(F32)
+        angle = (0.5 / math.pi) * gamma_ref[pos_y, layer]
+        inner(layer, False)
         pl.semaphore_wait(credit, 1)
 
         def back_send(i, carry):
@@ -343,7 +389,7 @@
                 own_im = work[1, core, ks, rows, :]
                 oth_re = recv[0, ks, rows, :]
                 oth_im = recv[1, ks, rows, :]
-                lam = mix_pair(own_re, own_im, oth_re, oth_im, cos_b, -sin_b)
+                lam = mix_pair(own_re, own_im, oth_re, oth_im, cos_b, sin_b)
                 lams = {0: lam[:2], 1: lam[2:]}
                 phi = []
                 costs = []
@@ -354,14 +400,15 @@
                     sin_p, cos_p = sincos(angle * cost_v)
                     waves.append((sin_p, cos_p))
                     if layer == 0:
-                        scale = 2.0 ** (-0.5 * (LOCAL + 1))
-                        phi.append((cos_p * scale, sin_p * -scale))
+                        real, imag = frame(lane_ones + core + side)
+                        phi.append((cos_p * real + sin_p * imag, cos_p * imag - sin_p * real))
                     else:
                         phi.append((phis[layer - 1, 0, side, ks, rows, :], phis[layer - 1, 1, side, ks, rows, :]))
                 for side in range(2):
                     lam_re, lam_im = lams[side]
                     gamma_sum = gamma_sum + jnp.sum(costs[side] * (lam_re * phi[side][1] - lam_im * phi[side][0]), axis=0)
-                    beta_sum = beta_sum + jnp.sum(lam_re * phi[1 - side][1] - lam_im * phi[1 - side][0], axis=0)
+                    cross = jnp.sum(lam_re * phi[1 - side][0] + lam_im * phi[1 - side][1], axis=0)
+                    beta_sum = beta_sum + cross if side == 0 else beta_sum - cross
                     if layer > 0:
                         sin_p, cos_p = waves[side]
                         where = core if side == 0 else other
@@ -371,7 +418,7 @@
 
             zero = jnp.zeros((CH, LN), F32)
             beta_sum, gamma_sum = lax.fori_loop(0, NK // KG, point, (zero, zero))
-            acc[1 + layer] += beta_sum
+            acc[1 + layer] += beta_sum * (1 - 2 * core).astype(F32)
             acc[4 + layer] += 2.0 * gamma_sum
             if layer > 0:
                 first_rows(i, False)
@@ -410,12 +457,15 @@
                 pltpu.VMEM((2, 2, NK, RB, LN), F32),
                 pltpu.VMEM((2, 2, NK, RB, LN), F32),
                 pltpu.VMEM((2, NK, RB, LN), F32),
-                pltpu.VMEM((3, 2, NK, RB, 2 * LN), F32),
+                pltpu.VMEM((3, 2, 2, NK, RB, LN), F32),
                 pltpu.VMEM((2, 2, 2, NK, RB, LN), F32),
                 pltpu.VMEM((768, 256), BF16),
-                pltpu.VMEM((2, 2, RB, LN), F32),
-                pltpu.VMEM((2, 10, 8, 256), F32),
-                pltpu.VMEM((8, 256), F32),
+                pltpu.VMEM((256, 256), BF16),
+                pltpu.VMEM((RB, LN), F32),
+                pltpu.VMEM((RB, LN), F32),
+                pltpu.VMEM((2, 256, 768), BF16),
+                pltpu.VMEM((2, 10, 8, LN), F32),
+                pltpu.VMEM((8, LN), F32),
                 pltpu.VMEM((8, 8, LN), F32),
                 pltpu.VMEM((8, LN), F32),
                 pltpu.VMEM((2, 2, 8, LN), F32),

time: 272 us -> 244 us (0.90)
  Pallas kernels: 268 us -> 240 us
    pallas_call x1, Pallas kernels: 268 us -> 240 us  [device_fn(): pl.pallas_call(kernel, out_shape=jax.ShapeDtypeStruct((2, 8, LN), F32), i...]
where the time goes in v2:
time: 244 us
  Pallas kernels  240 us (98%)
  local copies, waits for them, and re-layouts  2.65 us (1%)
    pallas_call x1, Pallas kernels, device_fn(): pl.pallas_call(kernel, out_shape=jax.ShapeDtypeStruct((2, 8, LN), F32), i...  240 us

profile of v2, /device:TPU:0, one launch (start us, length us, event | category | flops | bytes accessed | tf_op | source)
XLA Modules:
  0.0 243.6 jit_solution(3177969418715572266)
XLA Ops:
  0.6 240.3 %shard_map.50 = f32[2,8,128]{2,1,0:T(8,128)} custom-call(f32[16,128,128]{2,1,0:T(8,128)} %bitcast.1, f32[2,3]{1,0:T(2,128)} %gamma_ref.1, f32[2,3]{1,0:T(2,128)} %beta_ref.1), custom_call_target="tpu_custom_call" | custom-call | tf_op jit(solution)/shard_map/pallas_call | solution.py:451
  240.9 1.3 slice_reduce_fusion.1
  242.2 1.3 slice_reduce_fusion

commit v3 on v2

--- a/solution.py
+++ b/solution.py
@@ -64,7 +64,7 @@
     return high, mid, (rest - mid.astype(F32)).astype(BF16)
 
 
-def kernel(cost_ref, gamma_ref, beta_ref, out_ref, cost_all, work, recv, hats, phis, rot, flip, tmp, tmp2, lhs, dtab, wtab, acc, part, peers,
+def kernel(cost_ref, gamma_ref, beta_ref, out_ref, cost_all, work, recv, hats, phis, waves, rot, flip, tmp, lhs, dtab, wtab, acc, part, peers,
            own_s, own_r, rel_s, rel_r, core_s, core_r, ex_s, ex_r, fin_s, fin_r, credit):
     pos_y = lax.axis_index('qy')
     pos_b = lax.axis_index('qx')
@@ -74,12 +74,17 @@
     near_core = {'qy': pos_y, 'qx': pos_x * 2 + other}
     near_x = {'qy': pos_y, 'qx': (1 - pos_x) * 2 + core}
     near_y = {'qy': 1 - pos_y, 'qx': pos_b}
-    near_yc = {'qy': 1 - pos_y, 'qx': pos_x * 2 + other}
+    others = []
+    for d in range(1, 8):
+        to_y = 1 - pos_y if d & 4 else pos_y
+        to_x = 1 - pos_x if d & 2 else pos_x
+        to_core = other if d & 1 else core
+        others.append({'qy': to_y, 'qx': to_x * 2 + to_core})
 
     barrier = pltpu.get_barrier_semaphore()
-    for dev in (near_core, near_x, near_y, near_yc):
+    for dev in others:
         pl.semaphore_signal(barrier, inc=1, device_id=dev, device_id_type=MESH)
-    pl.semaphore_wait(barrier, 4)
+    pl.semaphore_wait(barrier, 7)
 
     def slot(block_y, block_x, block_core, chunk):
         return cost_all.at[block_y, block_x, pl.ds(block_core * 16 + chunk * GC, GC)]
@@ -176,9 +181,7 @@
         return real[None] * scale, imag[None] * scale
 
     def cost_half(layout, half, ks, rows):
-        if layout == 0:
-            return cost_all[core, half, ks, rows, :]
-        return cost_all[half, core, ks, rows, :]
+        return cost_all[(1 - layout) * core + layout * half, (1 - layout) * half + layout * core, ks, rows, :]
 
     def radix32(src, dst):
         dst[...] = butterfly(src[...], range(5))
@@ -198,7 +201,8 @@
         pops = [bin(m).count('1') for m in range(16)]
         return [jnp.concatenate([dtab[n, pop_i + pop] for pop in pops], axis=0) for n in range(2)]
 
-    def stage_in(i, slot, layer, forward):
+    def stage_in(i, slot, layer, forward, mine):
+        t = i - 16 * pos_x
         if forward:
             cos_d, sin_d = row_wave(i)
         for half in range(2):
@@ -211,8 +215,8 @@
             re_v, im_v = pair
             if forward:
                 pair = [re_v * cos_d + im_v * sin_d, im_v * cos_d - re_v * sin_d]
-            else:
-                prod = re_v * hats[layer, 1, half, i] - im_v * hats[layer, 0, half, i]
+            elif mine:
+                prod = re_v * hats[layer, 1, half, t] - im_v * hats[layer, 0, half, t]
                 sums = [None] * 5
                 for m in range(16):
                     pop = bin(m).count('1')
@@ -226,49 +230,70 @@
                 for n, piece in enumerate(split(pair[ri])):
                     lhs[slot, pl.ds(RB * ri, RB), pl.ds(2 * LN * n + LN * half, LN)] = piece
 
-    def stage_out(i, slot, layer, forward):
+    def stage_mm(i, slot, layer, forward, mine):
+        t = i - 16 * pos_x
         high = lhs[slot, :, 0:256]
         mid = lhs[slot, :, 256:512]
         low = lhs[slot, :, 512:768]
         table = [rot[0:256], rot[256:512], rot[512:768]]
         table = jnp.concatenate([table[0], table[1], table[2], table[0], table[1], table[0]], axis=0)
         prod = jnp.dot(jnp.concatenate([high, high, high, mid, mid, low], axis=1), table, preferred_element_type=F32)
-        if not forward:
+        if not forward and mine:
             turned = jnp.dot(jnp.concatenate([high, mid, low], axis=1), jnp.concatenate([flip[...]] * 3, axis=0), preferred_element_type=F32)
             total = None
             for half in range(2):
                 for ri in range(2):
-                    piece = turned[RB * ri:RB * ri + RB, LN * half:LN * half + LN] * hats[layer, ri, half, i]
+                    piece = turned[RB * ri:RB * ri + RB, LN * half:LN * half + LN] * hats[layer, ri, half, t]
                     piece = jnp.sum(piece.reshape(16, 8, LN), axis=0)
                     total = piece if total is None else total + piece
             acc[1 + layer] -= total
+        return prod
+
+    def stage_out(prod, i, layer, forward, mine):
+        t = i - 16 * pos_x
+        if not forward:
             cos_d, sin_d = row_wave(i)
         for half in range(2):
             re_v = prod[:RB, LN * half:LN * half + LN]
             im_v = prod[RB:, LN * half:LN * half + LN]
-            if forward:
-                hats[layer, 0, half, i] = re_v
-                hats[layer, 1, half, i] = im_v
-            else:
+            if forward and mine:
+                hats[layer, 0, half, t] = re_v
+                hats[layer, 1, half, t] = im_v
+            if not forward:
                 re_v, im_v = re_v * cos_d + im_v * sin_d, im_v * cos_d - re_v * sin_d
             for ri, items in enumerate((re_v, im_v)):
                 items = butterfly(items.reshape(16, 8, LN), range(4)).reshape(8, 2, 8, LN)
                 for b6 in range(2):
-                    tmp2[64 * b6:64 * b6 + 64] = items[:, b6].reshape(64, LN)
-                items = [tmp2[pl.ds(m, 16, stride=8), :].reshape(2, 1, 8, LN) for m in range(8)]
+                    tmp[64 * b6:64 * b6 + 64] = items[:, b6].reshape(64, LN)
+                items = [tmp[pl.ds(m, 16, stride=8), :].reshape(2, 1, 8, LN) for m in range(8)]
                 items = butterfly(jnp.concatenate(items, axis=1).reshape(16, 8, LN), range(3))
                 work[ri, half, i] = items.reshape(RB, LN)
 
     def inner(layer, forward):
-        stage_in(0, 0, layer, forward)
-
-        def body(p, carry):
-            stage_out(p, 0, layer, forward)
-            stage_in(p + 1, 0, layer, forward)
-            return carry
-
-        lax.fori_loop(0, NK - 1, body, 0)
-        stage_out(NK - 1, 0, layer, forward)
+        def body(mine):
+            def both(i, slot):
+                prod = stage_mm(i, slot, layer, forward, mine)
+                stage_in(i + 1, 1 - slot, layer, forward, mine)
+                stage_out(prod, i, layer, forward, mine)
+
+            def two(p, carry):
+                i = start + 2 * p
+                both(i, 0)
+                both(i + 1, 1)
+                return carry
+            start = first if mine else second
+            lax.fori_loop(0, 7, two, 0)
+            both(start + 14, 0)
+
+        first = 16 * pos_x
+        second = 16 - first
+        stage_in(first, 0, layer, forward, True)
+        body(True)
+        prod = stage_mm(first + 15, 1, layer, forward, True)
+        stage_in(second, 0, layer, forward, False)
+        stage_out(prod, first + 15, layer, forward, True)
+        body(False)
+        stage_out(stage_mm(second + 15, 1, layer, forward, False), second + 15, layer, forward, False)
 
     def last_rows(i):
         for ri in range(2):
@@ -290,79 +315,98 @@
             dst = chunk_of(work, ri, other, i)
             radix32(rchunk_of(ri, i) if received else dst, dst)
 
-    for layer in range(3):
+    def give_credit():
+        pl.semaphore_signal(credit, inc=1, device_id=near_core, device_id_type=MESH)
+
+    give_credit()
+
+    def send_layer(layer, initial, sin_b, cos_b):
         layout = layer % 2
+        angle = (0.5 / math.pi) * gamma_ref[pos_y, layer]
+
+        def send_body(mine):
+            def one(n, carry):
+                i = (n + 8 * pos_x) % NCH
+                if not initial:
+                    last_rows(i)
+
+                def point(kg, carry2):
+                    ks, rows = pieces(i, kg)
+                    here = pieces(n, kg)[1]
+                    state = []
+                    for half in range(2):
+                        sin_p, cos_p = sincos(angle * cost_half(layout, half, ks, rows))
+                        if initial:
+                            real, imag = frame(lane_ones + core + half)
+                            re_v = cos_p * real + sin_p * imag
+                            im_v = cos_p * imag - sin_p * real
+                        else:
+                            re_v = work[0, half, ks, rows, :]
+                            im_v = work[1, half, ks, rows, :]
+                            re_v, im_v = re_v * cos_p + im_v * sin_p, im_v * cos_p - re_v * sin_p
+                            waves[layer - 1, 0, half, ks, rows, :] = cos_p
+                            waves[layer - 1, 1, half, ks, rows, :] = sin_p
+                            if mine:
+                                phis[layer - 1, 0, half, ks, here, :] = re_v
+                                phis[layer - 1, 1, half, ks, here, :] = im_v
+                        state += [re_v, im_v]
+                    state = mix_pair(*state, cos_b, sin_b)
+                    for half in range(2):
+                        for ri in range(2):
+                            work[ri, half, ks, rows, :] = state[2 * half + ri]
+                    return carry2
+
+                lax.fori_loop(0, NK // KG, point, 0)
+                exchange(i).start()
+                return carry
+            return one
+
+        lax.fori_loop(0, NCH // 2, send_body(True), 0)
+        lax.fori_loop(NCH // 2, NCH, send_body(False), 0)
+
+    def forward_layer(layer, carry):
         make_dtab(layer, 1.0)
         make_rot(layer, 1.0)
         sin_b, cos_b = half_angle(layer)
-        angle = (0.5 / math.pi) * gamma_ref[pos_y, layer]
-        if layer > 0:
-            pl.semaphore_wait(credit, 1)
-
-        def send_body(i, carry):
-            if layer > 0:
-                last_rows(i)
-
-            def point(kg, carry2):
-                ks, rows = pieces(i, kg)
-                state = []
-                for half in range(2):
-                    sin_p, cos_p = sincos(angle * cost_half(layout, half, ks, rows))
-                    if layer == 0:
-                        real, imag = frame(lane_ones + core + half)
-                        re_v = cos_p * real + sin_p * imag
-                        im_v = cos_p * imag - sin_p * real
-                    else:
-                        re_v = work[0, half, ks, rows, :]
-                        im_v = work[1, half, ks, rows, :]
-                        re_v, im_v = re_v * cos_p + im_v * sin_p, im_v * cos_p - re_v * sin_p
-                        phis[layer - 1, 0, half, ks, rows, :] = re_v
-                        phis[layer - 1, 1, half, ks, rows, :] = im_v
-                    state += [re_v, im_v]
-                state = mix_pair(*state, cos_b, sin_b)
-                for half in range(2):
-                    for ri in range(2):
-                        work[ri, half, ks, rows, :] = state[2 * half + ri]
-                return carry2
-
-            lax.fori_loop(0, NK // KG, point, 0)
-            exchange(i).start()
-            return carry
-
-        lax.fori_loop(0, NCH, send_body, 0)
-
-        def take_body(i, carry):
+        pl.semaphore_wait(credit, 1)
+
+        @pl.when(layer == 0)
+        def _():
+            send_layer(layer, True, sin_b, cos_b)
+
+        @pl.when(layer > 0)
+        def _():
+            send_layer(layer, False, sin_b, cos_b)
+
+        def take_body(n, carry2):
+            i = (n + 8 * pos_x) % NCH
             exchange(i).wait()
             first_rows(i, True)
-            return carry
+            return carry2
 
         lax.fori_loop(0, NCH, take_body, 0)
-        pl.semaphore_signal(credit, inc=1, device_id=near_core, device_id_type=MESH)
+        give_credit()
         inner(layer, True)
+        return carry
+
+    lax.fori_loop(0, 3, forward_layer, 0)
 
     def turn_body(i, carry):
-        last_rows(i)
-
-        def point(kg, total):
-            ks, rows = pieces(i, kg)
-            for half in range(2):
-                cost_v = cost_half(1, half, ks, rows)
-                re_v = work[0, half, ks, rows, :]
-                im_v = work[1, half, ks, rows, :]
-                lam_re = cost_v * re_v
-                lam_im = cost_v * im_v
-                work[0, half, ks, rows, :] = lam_re
-                work[1, half, ks, rows, :] = lam_im
-                total = total + jnp.sum(lam_re * re_v + lam_im * im_v, axis=0)
-            return total
-
-        acc[0] += lax.fori_loop(0, NK // KG, point, jnp.zeros((CH, LN), F32))
-        first_rows(i, False)
+        total = jnp.zeros((CH, LN), F32)
+        for half in range(2):
+            for ri in range(2):
+                ref = chunk_of(work, ri, half, i)
+                values = butterfly(ref[...], range(5))
+                lam = values * cost_half(1, half, slice(None), pl.ds(pl.multiple_of(i * CH, CH), CH))
+                total = total + jnp.sum(values * lam, axis=0)
+                ref[...] = butterfly(lam, range(5))
+        acc[0] += 0.5 * total
         return carry
 
     lax.fori_loop(0, NCH, turn_body, 0)
 
-    for layer in (2, 1, 0):
+    def backward_layer(back, carry0):
+        layer = 2 - back
         layout = layer % 2
         make_dtab(layer, -1.0)
         make_rot(layer, -1.0)
@@ -371,76 +415,94 @@
         angle = (0.5 / math.pi) * gamma_ref[pos_y, layer]
         inner(layer, False)
         pl.semaphore_wait(credit, 1)
-
-        def back_send(i, carry):
+        count = NCH // 2 + (NCH // 2) * ((layer + 1) // 2)
+
+        def back_send(n, carry):
+            i = (n + 8 * pos_x) % NCH
             last_rows(i)
             exchange(i).start()
             return carry
 
-        lax.fori_loop(0, NCH, back_send, 0)
-
-        def back_take(i, carry):
-            exchange(i).wait()
-
-            def point(kg, sums):
-                ks, rows = pieces(i, kg)
-                beta_sum, gamma_sum = sums
-                own_re = work[0, core, ks, rows, :]
-                own_im = work[1, core, ks, rows, :]
-                oth_re = recv[0, ks, rows, :]
-                oth_im = recv[1, ks, rows, :]
-                lam = mix_pair(own_re, own_im, oth_re, oth_im, cos_b, sin_b)
-                lams = {0: lam[:2], 1: lam[2:]}
-                phi = []
-                costs = []
-                waves = []
-                for side in (core, other):
-                    cost_v = cost_half(layout, side, ks, rows)
-                    costs.append(cost_v)
-                    sin_p, cos_p = sincos(angle * cost_v)
-                    waves.append((sin_p, cos_p))
-                    if layer == 0:
-                        real, imag = frame(lane_ones + core + side)
-                        phi.append((cos_p * real + sin_p * imag, cos_p * imag - sin_p * real))
-                    else:
-                        phi.append((phis[layer - 1, 0, side, ks, rows, :], phis[layer - 1, 1, side, ks, rows, :]))
-                for side in range(2):
-                    lam_re, lam_im = lams[side]
-                    gamma_sum = gamma_sum + jnp.sum(costs[side] * (lam_re * phi[side][1] - lam_im * phi[side][0]), axis=0)
-                    cross = jnp.sum(lam_re * phi[1 - side][0] + lam_im * phi[1 - side][1], axis=0)
-                    beta_sum = beta_sum + cross if side == 0 else beta_sum - cross
-                    if layer > 0:
-                        sin_p, cos_p = waves[side]
-                        where = core if side == 0 else other
-                        work[0, where, ks, rows, :] = lam_re * cos_p - lam_im * sin_p
-                        work[1, where, ks, rows, :] = lam_im * cos_p + lam_re * sin_p
-                return beta_sum, gamma_sum
-
-            zero = jnp.zeros((CH, LN), F32)
-            beta_sum, gamma_sum = lax.fori_loop(0, NK // KG, point, (zero, zero))
-            acc[1 + layer] += beta_sum * (1 - 2 * core).astype(F32)
-            acc[4 + layer] += 2.0 * gamma_sum
-            if layer > 0:
-                first_rows(i, False)
-            return carry
-
-        lax.fori_loop(0, NCH, back_take, 0)
-        if layer > 0:
-            pl.semaphore_signal(credit, inc=1, device_id=near_core, device_id_type=MESH)
+        lax.fori_loop(0, count, back_send, 0)
+
+        def back_take(mine, final):
+            def one(n, carry):
+                i = (n + 8 * pos_x) % NCH
+                exchange(i).wait()
+
+                def point(kg, sums):
+                    ks, rows = pieces(i, kg)
+                    here = pieces(n, kg)[1]
+                    beta_sum, gamma_sum = sums
+                    own_re = work[0, core, ks, rows, :]
+                    own_im = work[1, core, ks, rows, :]
+                    oth_re = recv[0, ks, rows, :]
+                    oth_im = recv[1, ks, rows, :]
+                    lam = mix_pair(own_re, own_im, oth_re, oth_im, cos_b, sin_b)
+                    lams = (lam[:2], lam[2:])
+                    if mine:
+                        phi = []
+                        costs = []
+                        for side in (core, other):
+                            cost_v = cost_half(layout, side, ks, rows)
+                            costs.append(cost_v)
+                            if final:
+                                sin_p, cos_p = sincos(angle * cost_v)
+                                real, imag = frame(lane_ones + core + side)
+                                phi.append((cos_p * real + sin_p * imag, cos_p * imag - sin_p * real))
+                            else:
+                                phi.append((phis[layer - 1, 0, side, ks, here, :], phis[layer - 1, 1, side, ks, here, :]))
+                        for side in range(2):
+                            lam_re, lam_im = lams[side]
+                            gamma_sum = gamma_sum + jnp.sum(costs[side] * (lam_re * phi[side][1] - lam_im * phi[side][0]), axis=0)
+                            cross = jnp.sum(lam_re * phi[1 - side][0] + lam_im * phi[1 - side][1], axis=0)
+                            beta_sum = beta_sum + cross if side == 0 else beta_sum - cross
+                    if not final:
+                        for side, where in enumerate((core, other)):
+                            lam_re, lam_im = lams[side]
+                            cos_p = waves[layer - 1, 0, where, ks, rows, :]
+                            sin_p = waves[layer - 1, 1, where, ks, rows, :]
+                            work[0, where, ks, rows, :] = lam_re * cos_p - lam_im * sin_p
+                            work[1, where, ks, rows, :] = lam_im * cos_p + lam_re * sin_p
+                    return beta_sum, gamma_sum
+
+                zero = jnp.zeros((CH, LN), F32)
+                beta_sum, gamma_sum = lax.fori_loop(0, NK // KG, point, (zero, zero))
+                if mine:
+                    acc[1 + layer] += beta_sum * (1 - 2 * core).astype(F32)
+                    acc[4 + layer] += 2.0 * gamma_sum
+                if not final:
+                    first_rows(i, False)
+                return carry
+            return one
+
+        @pl.when(layer > 0)
+        def _():
+            lax.fori_loop(0, NCH // 2, back_take(True, False), 0)
+            lax.fori_loop(NCH // 2, NCH, back_take(False, False), 0)
+
+        @pl.when(layer == 0)
+        def _():
+            lax.fori_loop(0, NCH // 2, back_take(True, True), 0)
+
+        give_credit()
+        return carry0
+
+    lax.fori_loop(0, 3, backward_layer, 0)
+    pl.semaphore_wait(credit, 1)
 
     order = (0, 4, 5, 6, 1, 2, 3)
     rows = [jnp.sum(acc[q], axis=0, keepdims=True) for q in order]
     part[...] = jnp.concatenate(rows + [jnp.zeros((1, LN), F32)], axis=0)
-    peers[pos_y, core] = part[...]
-    fins = [push(part, peers.at[pos_y, core], fin_s.at[0], fin_r.at[0], near_core),
-            push(part, peers.at[pos_y, core], fin_s.at[1], fin_r.at[1], near_y),
-            push(part, peers.at[pos_y, core], fin_s.at[2], fin_r.at[2], near_yc)]
+    peers[pos_y, pos_b] = part[...]
+    fins = [push(part, peers.at[pos_y, pos_b], fin_s.at[n], fin_r.at[n], dev) for n, dev in enumerate(others)]
     for copy in fins:
         copy.start()
     for copy in fins:
         copy.wait()
-    for s in range(2):
-        out_ref[s] = jnp.broadcast_to(jnp.sum(peers[s, 0] + peers[s, 1], axis=1, keepdims=True), (8, LN))
+    for n in range(2):
+        total = peers[n, 0] + peers[n, 1] + peers[n, 2] + peers[n, 3]
+        out_ref[n] = jnp.broadcast_to(jnp.sum(total, axis=1, keepdims=True), (8, LN))
 
 
 def solution(mesh):
@@ -457,20 +519,20 @@
                 pltpu.VMEM((2, 2, NK, RB, LN), F32),
                 pltpu.VMEM((2, 2, NK, RB, LN), F32),
                 pltpu.VMEM((2, NK, RB, LN), F32),
-                pltpu.VMEM((3, 2, 2, NK, RB, LN), F32),
+                pltpu.VMEM((3, 2, 2, NK // 2, RB, LN), F32),
+                pltpu.VMEM((2, 2, 2, NK, RB // 2, LN), F32),
                 pltpu.VMEM((2, 2, 2, NK, RB, LN), F32),
                 pltpu.VMEM((768, 256), BF16),
                 pltpu.VMEM((256, 256), BF16),
-                pltpu.VMEM((RB, LN), F32),
                 pltpu.VMEM((RB, LN), F32),
                 pltpu.VMEM((2, 256, 768), BF16),
                 pltpu.VMEM((2, 10, 8, LN), F32),
                 pltpu.VMEM((8, LN), F32),
                 pltpu.VMEM((8, 8, LN), F32),
                 pltpu.VMEM((8, LN), F32),
-                pltpu.VMEM((2, 2, 8, LN), F32),
+                pltpu.VMEM((2, 4, 8, LN), F32),
                 dma((2, 4)), dma((2, 4)), dma((4,)), dma((4,)), dma((4, 4)), dma((4, 4)),
-                dma((NCH,)), dma((NCH,)), dma((3,)), dma((3,)),
+                dma((NCH,)), dma((NCH,)), dma((7,)), dma((7,)),
                 pltpu.SemaphoreType.REGULAR,
             ],
             compiler_params=pltpu.CompilerParams(collective_id=0, has_side_effects=True, vmem_limit_bytes=67043328),

time: 244 us -> 216 us (0.89)
  Pallas kernels: 240 us -> 213 us
    pallas_call x1, Pallas kernels: 240 us -> 213 us  [device_fn(): pl.pallas_call(kernel, out_shape=jax.ShapeDtypeStruct((2, 8, LN), F32), i...]
where the time goes in v3:
time: 216 us
  Pallas kernels  213 us (99%)
  local copies, waits for them, and re-layouts  2.65 us (1%)
    pallas_call x1, Pallas kernels, device_fn(): pl.pallas_call(kernel, out_shape=jax.ShapeDtypeStruct((2, 8, LN), F32), i...  213 us

profile of v3, /device:TPU:0, one launch (start us, length us, event | category | flops | bytes accessed | tf_op | source)
XLA Modules:
  0.0 216.2 jit_solution(15920804930565724843)
XLA Ops:
  0.6 212.9 %shard_map.50 = f32[2,8,128]{2,1,0:T(8,128)} custom-call(f32[16,128,128]{2,1,0:T(8,128)} %bitcast.1, f32[2,3]{1,0:T(2,128)} %gamma_ref.1, f32[2,3]{1,0:T(2,128)} %beta_ref.1), custom_call_target="tpu_custom_call" | custom-call | tf_op jit(solution)/shard_map/pallas_call | solution.py:513
  213.5 1.3 slice_reduce_fusion.1
  214.8 1.3 slice_reduce_fusion

commit v4 on v3

--- a/solution.py
+++ b/solution.py
@@ -64,7 +64,7 @@
     return high, mid, (rest - mid.astype(F32)).astype(BF16)
 
 
-def kernel(cost_ref, gamma_ref, beta_ref, out_ref, cost_all, work, recv, hats, phis, waves, rot, flip, tmp, lhs, dtab, wtab, acc, part, peers,
+def kernel(cost_ref, gamma_ref, beta_ref, energy_ref, grad_ref, cost_all, work, recv, hats, phis, waves, rot, flip, tmp, lhs, dtab, wtab, acc, part, peers,
            own_s, own_r, rel_s, rel_r, core_s, core_r, ex_s, ex_r, fin_s, fin_r, credit):
     pos_y = lax.axis_index('qy')
     pos_b = lax.axis_index('qx')
@@ -270,30 +270,31 @@
                 work[ri, half, i] = items.reshape(RB, LN)
 
     def inner(layer, forward):
+        slots = (0, 1, 0, 1, 2)
+
         def body(mine):
-            def both(i, slot):
+            def both(i, slot, after):
                 prod = stage_mm(i, slot, layer, forward, mine)
-                stage_in(i + 1, 1 - slot, layer, forward, mine)
+                stage_in(i + 1, after, layer, forward, mine)
                 stage_out(prod, i, layer, forward, mine)
 
-            def two(p, carry):
-                i = start + 2 * p
-                both(i, 0)
-                both(i + 1, 1)
+            def trip(p, carry):
+                i = start + 5 * p
+                for n in range(5):
+                    both(i + n, slots[n], slots[(n + 1) % 5])
                 return carry
             start = first if mine else second
-            lax.fori_loop(0, 7, two, 0)
-            both(start + 14, 0)
+            lax.fori_loop(0, 3, trip, 0)
 
         first = 16 * pos_x
         second = 16 - first
         stage_in(first, 0, layer, forward, True)
         body(True)
-        prod = stage_mm(first + 15, 1, layer, forward, True)
+        prod = stage_mm(first + 15, 0, layer, forward, True)
         stage_in(second, 0, layer, forward, False)
         stage_out(prod, first + 15, layer, forward, True)
         body(False)
-        stage_out(stage_mm(second + 15, 1, layer, forward, False), second + 15, layer, forward, False)
+        stage_out(stage_mm(second + 15, 0, layer, forward, False), second + 15, layer, forward, False)
 
     def last_rows(i):
         for ri in range(2):
@@ -502,7 +503,12 @@
         copy.wait()
     for n in range(2):
         total = peers[n, 0] + peers[n, 1] + peers[n, 2] + peers[n, 3]
-        out_ref[n] = jnp.broadcast_to(jnp.sum(total, axis=1, keepdims=True), (8, LN))
+        for q in range(7):
+            value = jnp.sum(total[q:q + 1])
+            if q == 0:
+                energy_ref[n] = value
+            else:
+                grad_ref[n, q - 1] = value
 
 
 def solution(mesh):
@@ -510,11 +516,11 @@
         vmem = pl.BlockSpec(memory_space=pltpu.VMEM)
         smem = pl.BlockSpec(memory_space=pltpu.SMEM)
         dma = pltpu.SemaphoreType.DMA
-        out = pl.pallas_call(
+        return pl.pallas_call(
             kernel,
-            out_shape=jax.ShapeDtypeStruct((2, 8, LN), F32),
+            out_shape=(jax.ShapeDtypeStruct((2,), F32), jax.ShapeDtypeStruct((2, 6), F32)),
             in_specs=[vmem, smem, smem],
-            out_specs=vmem,
+            out_specs=(smem, smem),
             scratch_shapes=[
                 pltpu.VMEM((2, 2, NK, RB, LN), F32),
                 pltpu.VMEM((2, 2, NK, RB, LN), F32),
@@ -525,7 +531,7 @@
                 pltpu.VMEM((768, 256), BF16),
                 pltpu.VMEM((256, 256), BF16),
                 pltpu.VMEM((RB, LN), F32),
-                pltpu.VMEM((2, 256, 768), BF16),
+                pltpu.VMEM((3, 256, 768), BF16),
                 pltpu.VMEM((2, 10, 8, LN), F32),
                 pltpu.VMEM((8, LN), F32),
                 pltpu.VMEM((8, 8, LN), F32),
@@ -537,7 +543,6 @@
             ],
             compiler_params=pltpu.CompilerParams(collective_id=0, has_side_effects=True, vmem_limit_bytes=67043328),
         )(cost.reshape(16, RB, LN), gamma, beta)
-        return out[:, 0, 0], out[:, 1:7, 0]
 
     cost_spec = P(('inst', 'qy', 'qx'))
     angle_spec = P('inst', None)

time: 216 us -> 209 us (0.968)
  Pallas kernels: 213 us -> 206 us
    pallas_call x1, Pallas kernels: 213 us -> 206 us  [device_fn(): pl.pallas_call(kernel, out_shape=(jax.ShapeDtypeStruct((2,), F32), jax.Sh...]
    slice x2 -> x0, local copies, waits for them, and re-layouts: 2.65 us -> none  [device_fn(): return (out[:, 0, 0], out[:, 1:7, 0])]
where the time goes in v4:
time: 209 us
  Pallas kernels  206 us (99%)
    pallas_call x1, Pallas kernels, device_fn(): pl.pallas_call(kernel, out_shape=(jax.ShapeDtypeStruct((2,), F32), jax.Sh...  206 us

profile of v4, /device:TPU:0, one launch (start us, length us, event | category | flops | bytes accessed | tf_op | source)
XLA Modules:
  0.0 209.0 jit_solution(11371794835908389632)
XLA Ops:
  0.6 206.4 %shard_map.50 = (f32[2]{0:T(128)}, f32[2,6]{1,0:T(2,128)}) custom-call(f32[16,128,128]{2,1,0:T(8,128)} %bitcast.1, f32[2,3]{1,0:T(2,128)} %gamma_ref.1, f32[2,3]{1,0:T(2,128)} %beta_ref.1), custom_call_target="tpu_custom_call" | custom-call | tf_op jit(solution)/shard_map/pallas_call | solution.py:519
  207.1 0.0 copy-start.1
  207.1 0.6 copy-done.1
  207.7 0.0 copy-start
  207.7 0.5 copy.7
  208.2 0.2 copy-done
  208.4 0.6 copy.8
Async XLA Ops:
  207.1 0.6 copy-start.1
  207.7 0.7 copy-start

commit v5 on v4

--- a/solution.py
+++ b/solution.py
@@ -15,7 +15,7 @@
 CH = 8
 NCH = RB // CH
 GC = 4
-KG = 8
+KG = 4
 MESH = pl.DeviceIdType.MESH
 QUBITS = 21
 ROWQ = 12
@@ -235,9 +235,12 @@
         high = lhs[slot, :, 0:256]
         mid = lhs[slot, :, 256:512]
         low = lhs[slot, :, 512:768]
-        table = [rot[0:256], rot[256:512], rot[512:768]]
-        table = jnp.concatenate([table[0], table[1], table[2], table[0], table[1], table[0]], axis=0)
-        prod = jnp.dot(jnp.concatenate([high, high, high, mid, mid, low], axis=1), table, preferred_element_type=F32)
+        table = jnp.concatenate([rot[...], rot[0:512], rot[0:256]], axis=0)
+        parts = jnp.concatenate([high, high, high, mid, mid, low], axis=1)
+        prods = []
+        for ri in range(2):
+            prods.append(jnp.dot(parts[RB * ri:RB * ri + RB], table, preferred_element_type=F32))
+        prod = jnp.concatenate(prods, axis=0)
         if not forward and mine:
             turned = jnp.dot(jnp.concatenate([high, mid, low], axis=1), jnp.concatenate([flip[...]] * 3, axis=0), preferred_element_type=F32)
             total = None

time: 209 us -> 208 us (level)
  no operation moved by 1% of the time
where the time goes in v5:
time: 208 us
  Pallas kernels  205 us (99%)
    pallas_call x1, Pallas kernels, device_fn(): pl.pallas_call(kernel, out_shape=(jax.ShapeDtypeStruct((2,), F32), jax.Sh...  205 us

profile of v5, /device:TPU:0, one launch (start us, length us, event | category | flops | bytes accessed | tf_op | source)
XLA Modules:
  0.0 207.5 jit_solution(16649617412568180437)
XLA Ops:
  0.6 205.0 %shard_map.50 = (f32[2]{0:T(128)}, f32[2,6]{1,0:T(2,128)}) custom-call(f32[16,128,128]{2,1,0:T(8,128)} %bitcast.1, f32[2,3]{1,0:T(2,128)} %gamma_ref.1, f32[2,3]{1,0:T(2,128)} %beta_ref.1), custom_call_target="tpu_custom_call" | custom-call | tf_op jit(solution)/shard_map/pallas_call | solution.py:522
  205.7 0.0 copy-start.1
  205.7 0.6 copy-done.1
  206.3 0.0 copy-start
  206.3 0.5 copy.7
  206.8 0.2 copy-done
  207.0 0.6 copy.8
Async XLA Ops:
  205.7 0.6 copy-start.1
  206.3 0.7 copy-start
